TPU v7x, 32 devices: a whole 2x2x4 slice. The times are simulated.
32 devices in a mesh: dp: 16 (over z, x, core), tensor: 2 (over y).
Axes of the slice: x: 2, y: 2, z: 4, core: 2. Of those that a mesh axis runs over, the one named last changes fastest.
Arguments:
- states: float32 [24576, 1536], P(('dp', 'tensor')), may hold values from -6 to 6
- text_states: float32 [16, 64, 1536], P('dp'), may hold values from -6 to 6
- norm_gains: float32 [3, 1536], P(None, 'dp'), may hold values from 0.25 to 1.75
- norm_biases: float32 [3, 1536], P(None, 'dp'), may hold values from -3 to 3
- self_qkv: float32 [1536, 3, 1536], P('dp', None, 'tensor'), may hold values from -0.15625 to 0.15625
- self_out: float32 [1536, 1536], P('tensor', 'dp'), may hold values from -1.25 to 1.25
- cross_query: float32 [1536, 1536], P('dp', 'tensor'), may hold values from -0.15625 to 0.15625
- cross_kv: float32 [1536, 2, 1536], P('dp', None, 'tensor'), may hold values from -0.15625 to 0.15625
- cross_out: float32 [1536, 1536], P('tensor', 'dp'), may hold values from -1.25 to 1.25
- mlp_up: float32 [1536, 6144], P('dp', 'tensor'), may hold values from -0.15625 to 0.15625
- mlp_down: float32 [6144, 1536], P('tensor', 'dp'), may hold values from -0.078125 to 0.078125
- out_grad: float32 [24576, 1536], P(('dp', 'tensor')), may hold values from -6 to 6
Outputs:
- layer_out: float32 [24576, 1536], P(('dp', 'tensor'))
- states_grad: float32 [24576, 1536], P(('dp', 'tensor'))
- text_grad: float32 [16, 64, 1536], P('dp')
- gains_grad: float32 [3, 1536], P(None, 'dp')
- biases_grad: float32 [3, 1536], P(None, 'dp')
- self_qkv_grad: float32 [1536, 3, 1536], P('dp', None, 'tensor')
- self_out_grad: float32 [1536, 1536], P('tensor', 'dp')
- cross_query_grad: float32 [1536, 1536], P('dp', 'tensor')
- cross_kv_grad: float32 [1536, 2, 1536], P('dp', None, 'tensor')
- cross_out_grad: float32 [1536, 1536], P('tensor', 'dp')
- mlp_up_grad: float32 [1536, 6144], P('dp', 'tensor')
- mlp_down_grad: float32 [6144, 1536], P('tensor', 'dp')
All inputs are finite; a program needn't handle non-finite values.
Results may differ from a plain program's by a relative error of at most 0.017.
The roundings to bfloat16 on the way count: a program that leaves them out, or rounds other values in their place, can miss the bound.
Values may be sent and summed in bfloat16 or wider, within the bound.
A program may use at most 384 MiB of HBM per device.

v0:
```python
import math

import jax
import jax.numpy as jnp
from jax import lax
from jax.sharding import PartitionSpec as P

HEAD_DIM = 64


EPSILON = 1e-05
MASKED = -1e30


def normalize(values, gain, shift):
    centre = jnp.mean(values, axis=1, keepdims=True)
    centred = values - centre
    spread = jnp.mean(centred * centred, axis=1, keepdims=True)
    return centred * lax.rsqrt(spread + EPSILON) * gain + shift


def activate(values):
    return jax.nn.gelu(values, approximate=False)


def gather_rows(local_rows):
    return lax.all_gather(local_rows, "tensor", axis=0, tiled=True)


def project_rows(operand, weight, leading):
    if leading:
        pattern = "tkc,cd->td"
    else:
        pattern = "tkc,dkc->td"
    return lax.psum_scatter(
        jnp.einsum(pattern, operand, weight, preferred_element_type=jnp.float32),
        "tensor",
        scatter_dimension=0,
        tiled=True,
    )


def score_block(query_block, keys, offset, causal):
    scale_factor = 1.0 / math.sqrt(query_block.shape[2])
    scores = (
        jnp.einsum("bhe,khe->hbk", query_block, keys, preferred_element_type=jnp.float32)
        * scale_factor
    )
    if causal:
        query_pos = offset + lax.broadcasted_iota(
            jnp.int32, (query_block.shape[0], keys.shape[0]), 0
        )
        key_pos = lax.broadcasted_iota(jnp.int32, (query_block.shape[0], keys.shape[0]), 1)
        scores = jnp.where((key_pos <= query_pos)[None], scores, MASKED)
    return scores


def attend(queries, keys, values, causal):
    length = queries.shape[0]
    block = min(512, length)

    def one_block(number):
        offset = number * block
        query_block = lax.dynamic_slice_in_dim(queries, offset, block, 0)
        scores = score_block(query_block, keys, offset, causal)
        highest = jnp.max(scores, axis=2, keepdims=True)
        raised = jnp.exp(scores - highest)
        totals = jnp.sum(raised, axis=2, keepdims=True)
        weights = (raised / totals).astype(jnp.bfloat16)
        mixed = jnp.einsum("hbk,khe->bhe", weights, values, preferred_element_type=jnp.float32)
        return (mixed.astype(jnp.bfloat16), (highest + jnp.log(totals))[:, :, 0])

    mixed, log_totals = lax.map(one_block, jnp.arange(length // block, dtype=jnp.int32))
    return (mixed.reshape(queries.shape), log_totals)


def attend_back(queries, keys, values, log_totals, out_grads, causal):
    length = queries.shape[0]
    block = min(512, length)
    scale_factor = 1.0 / math.sqrt(queries.shape[2])

    def one_block(carried, number):
        key_grads, value_grads = carried
        offset = number * block
        query_block = lax.dynamic_slice_in_dim(queries, offset, block, 0)
        grad_block = lax.dynamic_slice_in_dim(out_grads, offset, block, 0)
        scores = score_block(query_block, keys, offset, causal)
        probs = jnp.exp(scores - log_totals[number][:, :, None])
        prob_grads = jnp.einsum(
            "bhe,khe->hbk", grad_block, values, preferred_element_type=jnp.float32
        )
        centre = jnp.sum(probs * prob_grads, axis=2, keepdims=True)
        score_grads = (probs * (prob_grads - centre)).astype(jnp.bfloat16)
        query_grads = (
            jnp.einsum("hbk,khe->bhe", score_grads, keys, preferred_element_type=jnp.float32)
            * scale_factor
        )
        key_grads = (
            key_grads
            + jnp.einsum(
                "hbk,bhe->khe", score_grads, query_block, preferred_element_type=jnp.float32
            )
            * scale_factor
        )
        value_grads = value_grads + jnp.einsum(
            "hbk,bhe->khe",
            probs.astype(jnp.bfloat16),
            grad_block,
            preferred_element_type=jnp.float32,
        )
        return ((key_grads, value_grads), query_grads)

    empty = jnp.zeros(keys.shape, jnp.float32)
    (key_grads, value_grads), query_grads = lax.scan(
        one_block, (empty, empty), jnp.arange(length // block, dtype=jnp.int32)
    )
    return (query_grads.reshape(queries.shape), key_grads, value_grads)


def on_device(
    states,
    text_states,
    norm_gains,
    norm_biases,
    self_qkv,
    self_out,
    cross_query,
    cross_kv,
    cross_out,
    mlp_up,
    mlp_down,
    out_grad,
):
    lane_count = self_qkv.shape[2]
    head_count = lane_count // HEAD_DIM
    fetched = (
        lax.all_gather(norm_gains.astype(jnp.bfloat16), "dp", axis=1, tiled=True),
        lax.all_gather(norm_biases.astype(jnp.bfloat16), "dp", axis=1, tiled=True),
        lax.all_gather(self_qkv.astype(jnp.bfloat16), "dp", axis=0, tiled=True),
        lax.all_gather(self_out.astype(jnp.bfloat16), "dp", axis=1, tiled=True),
        lax.all_gather(cross_query.astype(jnp.bfloat16), "dp", axis=0, tiled=True),
        lax.all_gather(cross_kv.astype(jnp.bfloat16), "dp", axis=0, tiled=True),
        lax.all_gather(cross_out.astype(jnp.bfloat16), "dp", axis=1, tiled=True),
        lax.all_gather(mlp_up.astype(jnp.bfloat16), "dp", axis=0, tiled=True),
        lax.all_gather(mlp_down.astype(jnp.bfloat16), "dp", axis=1, tiled=True),
    )
    gains_low, biases_low, w_qkv, w_self_out, w_query, w_kv, w_cross_out, w_up, w_down = fetched
    gains = gains_low.astype(jnp.float32)
    biases = biases_low.astype(jnp.float32)

    def split_heads(block):
        return block.reshape(block.shape[0], head_count, HEAD_DIM)

    def as_rows(block):
        return block.reshape(block.shape[0], 1, block.shape[-1])

    def as_columns(weight):
        return weight.reshape(weight.shape[0], 1, weight.shape[1])

    def norm_back(values, which, grads):
        _, pull = jax.vjp(normalize, values, gains[which], biases[which])
        return pull(grads)

    normed_one = gather_rows(normalize(states, gains[0], biases[0]).astype(jnp.bfloat16))
    triple = jnp.einsum(
        "td,dkc->tkc", normed_one, w_qkv, preferred_element_type=jnp.float32
    ).astype(jnp.bfloat16)
    self_queries = split_heads(triple[:, 0])
    self_keys = split_heads(triple[:, 1])
    self_values = split_heads(triple[:, 2])
    self_mixed, self_totals = attend(self_queries, self_keys, self_values, True)
    self_flat = self_mixed.reshape(-1, lane_count)
    after_self = states + project_rows(as_rows(self_flat), w_self_out, True)
    normed_two = gather_rows(normalize(after_self, gains[1], biases[1]).astype(jnp.bfloat16))
    cross_queries = jnp.dot(normed_two, w_query, preferred_element_type=jnp.float32).astype(
        jnp.bfloat16
    )
    text_low = text_states[0].astype(jnp.bfloat16)
    text_pair = jnp.einsum(
        "td,dkc->tkc", text_low, w_kv, preferred_element_type=jnp.float32
    ).astype(jnp.bfloat16)
    text_keys = split_heads(text_pair[:, 0])
    text_values = split_heads(text_pair[:, 1])
    cross_mixed, cross_totals = attend(split_heads(cross_queries), text_keys, text_values, False)
    cross_flat = cross_mixed.reshape(-1, lane_count)
    after_cross = after_self + project_rows(as_rows(cross_flat), w_cross_out, True)
    normed_three = gather_rows(normalize(after_cross, gains[2], biases[2]).astype(jnp.bfloat16))
    hidden_pre = jnp.dot(normed_three, w_up, preferred_element_type=jnp.float32)
    hidden = activate(hidden_pre).astype(jnp.bfloat16)
    layer_out = after_cross + project_rows(as_rows(hidden), w_down, True)
    branch_grads = gather_rows(out_grad.astype(jnp.bfloat16))
    down_grad = jnp.einsum("tf,td->fd", hidden, branch_grads, preferred_element_type=jnp.float32)
    hidden_grad = jnp.einsum("td,fd->tf", branch_grads, w_down, preferred_element_type=jnp.float32)
    _, pull_act = jax.vjp(activate, hidden_pre)
    pre_grad = pull_act(hidden_grad)[0].astype(jnp.bfloat16)
    up_grad = jnp.einsum("td,tf->df", normed_three, pre_grad, preferred_element_type=jnp.float32)
    back_three = project_rows(as_rows(pre_grad), as_columns(w_up), False)
    rows_three, gain_three, shift_three = norm_back(after_cross, 2, back_three)
    cross_rows_grad = out_grad + rows_three
    cross_grads = gather_rows(cross_rows_grad.astype(jnp.bfloat16))
    cross_out_grad = jnp.einsum(
        "tc,td->cd", cross_flat, cross_grads, preferred_element_type=jnp.float32
    )
    cross_mixed_grad = jnp.einsum(
        "td,cd->tc", cross_grads, w_cross_out, preferred_element_type=jnp.float32
    ).astype(jnp.bfloat16)
    query_grad, text_key_grad, text_value_grad = attend_back(
        split_heads(cross_queries),
        text_keys,
        text_values,
        cross_totals,
        split_heads(cross_mixed_grad),
        False,
    )
    query_grad = query_grad.reshape(-1, lane_count).astype(jnp.bfloat16)
    pair_grad = jnp.stack(
        [text_key_grad.reshape(-1, lane_count), text_value_grad.reshape(-1, lane_count)], axis=1
    ).astype(jnp.bfloat16)
    query_weight_grad = jnp.einsum(
        "td,tc->dc", normed_two, query_grad, preferred_element_type=jnp.float32
    )
    kv_weight_grad = jnp.einsum(
        "td,tkc->dkc", text_low, pair_grad, preferred_element_type=jnp.float32
    )
    text_grad_part = jnp.einsum("tkc,dkc->td", pair_grad, w_kv, preferred_element_type=jnp.float32)
    back_two = project_rows(as_rows(query_grad), as_columns(w_query), False)
    rows_two, gain_two, shift_two = norm_back(after_self, 1, back_two)
    self_rows_grad = cross_rows_grad + rows_two
    self_grads = gather_rows(self_rows_grad.astype(jnp.bfloat16))
    self_out_grad = jnp.einsum(
        "tc,td->cd", self_flat, self_grads, preferred_element_type=jnp.float32
    )
    self_mixed_grad = jnp.einsum(
        "td,cd->tc", self_grads, w_self_out, preferred_element_type=jnp.float32
    ).astype(jnp.bfloat16)
    self_query_grad, self_key_grad, self_value_grad = attend_back(
        self_queries, self_keys, self_values, self_totals, split_heads(self_mixed_grad), True
    )
    triple_grad = jnp.stack(
        [
            self_query_grad.reshape(-1, lane_count),
            self_key_grad.reshape(-1, lane_count),
            self_value_grad.reshape(-1, lane_count),
        ],
        axis=1,
    ).astype(jnp.bfloat16)
    qkv_weight_grad = jnp.einsum(
        "td,tkc->dkc", normed_one, triple_grad, preferred_element_type=jnp.float32
    )
    back_one = project_rows(triple_grad, w_qkv, False)
    rows_one, gain_one, shift_one = norm_back(states, 0, back_one)
    states_grad = self_rows_grad + rows_one
    gain_parts = jnp.stack([gain_one, gain_two, gain_three])
    shift_parts = jnp.stack([shift_one, shift_two, shift_three])
    text_total, gain_total, shift_total = lax.psum(
        (text_grad_part, gain_parts, shift_parts), "tensor"
    )
    summed = (
        lax.psum_scatter(gain_total, "dp", scatter_dimension=1, tiled=True),
        lax.psum_scatter(shift_total, "dp", scatter_dimension=1, tiled=True),
        lax.psum_scatter(qkv_weight_grad, "dp", scatter_dimension=0, tiled=True),
        lax.psum_scatter(self_out_grad, "dp", scatter_dimension=1, tiled=True),
        lax.psum_scatter(query_weight_grad, "dp", scatter_dimension=0, tiled=True),
        lax.psum_scatter(kv_weight_grad, "dp", scatter_dimension=0, tiled=True),
        lax.psum_scatter(cross_out_grad, "dp", scatter_dimension=1, tiled=True),
        lax.psum_scatter(up_grad, "dp", scatter_dimension=0, tiled=True),
        lax.psum_scatter(down_grad, "dp", scatter_dimension=1, tiled=True),
    )
    (
        gain_sum,
        shift_sum,
        qkv_sum,
        self_out_sum,
        query_sum,
        kv_sum,
        cross_out_sum,
        up_sum,
        down_sum,
    ) = summed
    return (
        layer_out,
        states_grad,
        text_total[None],
        gain_sum,
        shift_sum,
        qkv_sum,
        self_out_sum,
        query_sum,
        kv_sum,
        cross_out_sum,
        up_sum,
        down_sum,
    )


def solution(mesh):
    placed = (
        P(("dp", "tensor"), None),
        P("dp", None, None),
        P(None, "dp"),
        P(None, "dp"),
        P("dp", None, "tensor"),
        P("tensor", "dp"),
        P("dp", "tensor"),
        P("dp", None, "tensor"),
        P("tensor", "dp"),
        P("dp", "tensor"),
        P("tensor", "dp"),
        P(("dp", "tensor"), None),
    )
    return jax.shard_map(
        on_device,
        mesh=mesh,
        in_specs=placed,
        out_specs=(
            P(("dp", "tensor"), None),
            P(("dp", "tensor"), None),
            P("dp", None, None),
            P(None, "dp"),
            P(None, "dp"),
            P("dp", None, "tensor"),
            P("tensor", "dp"),
            P("dp", "tensor"),
            P("dp", None, "tensor"),
            P("tensor", "dp"),
            P("dp", "tensor"),
            P("tensor", "dp"),
        ),
        check_vma=False,
    )
```

profile of v0, /device:TPU:1, one launch (start us, length us, event | category | flops | bytes accessed | tf_op | source)
XLA Modules:
  0.0 3402.8 jit_solution(17524411774453878501)
XLA Ops:
  14.2 23.0 all-gather.1
  37.9 17.4 all-gather
  63.1 58.8 %all-gather.16.cloned.1.call-done = bf16[1536,1536]{1,0:T(8,128)(2,1)} async-done(((bf16[768,1536]{1,0:T(8,128)(2,1)}), bf16[1536,1536]{1,0:T(8,128)(2,1)}) %all-gather.16.cloned.1.call-update) | async-done | bytes 4718608 | tf_op jit(solution)/shard_map/all_gather | solution.py:27
  121.9 69.5 %all-gather.18.cloned.1.call-done = bf16[1536,3,768]{2,0,1:T(8,128)(2,1)} async-done(((bf16[96,3,768]{2,0,1:T(8,128)(2,1)}), bf16[1536,3,768]{2,0,1:T(8,128)(2,1)}) %all-gather.18.cloned.1.call-update) | async-done | bytes 7077904 | tf_op jit(solution)/shard_map/all_gather | solution.py:139
  191.4 14.7 convolution_convert_fusion.1
  210.7 159.8 %while.54 = (s32[]{:T(128)}, bf16[3,512,12,64]{1,3,2,0:T(8,128)(2,1)}, f32[3,12,512]{2,1,0:T(8,128)S(1)}, s32[3]{0:T(128)S(1)}, bf16[1536,12,64]{0,2,1:T(8,128)(...) while((s32[]{:T(128)}, ...), condition=%wide.region_5.6_spmd, body=%wide.region_2.5_spmd.sunk | while | flops 2530339328 | bytes 132346064 | solution.py:73
  212.9 17.1 fusion.172
  230.1 17.5 fusion.173
  247.6 16.9 fusion.174
  266.2 16.9 fusion.172
  283.2 17.4 fusion.173
  300.5 16.9 fusion.174
  319.2 16.9 fusion.172
  336.1 17.4 fusion.173
  353.5 16.9 fusion.174
  390.0 106.3 %reduce-scatter.19.cloned.1.call-done = f32[768,1536]{1,0:T(8,128)} async-done(((f32[1536,1536]{1,0:T(8,128)}), f32[768,1536]{1,0:T(8,128)}) %reduce-scatter.19.cloned.1.call-update) | async-done | bytes 4718608 | tf_op jit(solution)/shard_map/reduce_scatter | solution.py:35
  506.0 46.8 %all-gather.26.cloned.1.call-done = bf16[1536,2,768]{2,0,1:T(8,128)(2,1)} async-done(((bf16[96,2,768]{2,0,1:T(8,128)(2,1)}), bf16[1536,2,768]{2,0,1:T(8,128)(2,1)}) %all-gather.26.cloned.1.call-update) | async-done | bytes 4718608 | tf_op jit(solution)/shard_map/all_gather | solution.py:142
  556.7 39.6 %all-gather.24.cloned.1.call-done = bf16[1536,768]{1,0:T(8,128)(2,1)} async-done(((bf16[96,768]{1,0:T(8,128)(2,1)}), bf16[1536,768]{1,0:T(8,128)(2,1)}) %all-gather.24.cloned.1.call-update) | async-done | bytes 2359312 | tf_op jit(solution)/shard_map/all_gather | solution.py:141
  596.4 62.9 %all-gather.22.cloned.1.call-done = bf16[1536,1536]{1,0:T(8,128)(2,1)} async-done(((bf16[768,1536]{1,0:T(8,128)(2,1)}), bf16[1536,1536]{1,0:T(8,128)(2,1)}) %all-gather.22.cloned.1.call-update) | async-done | bytes 4718608 | tf_op jit(solution)/shard_map/all_gather | solution.py:27
  684.6 20.5 all-gather.28.cloned.1.call-done
  717.3 106.7 %reduce-scatter.21.cloned.1.call-done = f32[768,1536]{1,0:T(8,128)} async-done(((f32[1536,1536]{1,0:T(8,128)}), f32[768,1536]{1,0:T(8,128)}) %reduce-scatter.21.cloned.1.call-update) | async-done | bytes 4718608 | tf_op jit(solution)/shard_map/reduce_scatter | solution.py:35
  838.3 70.0 %all-gather.32.cloned.1.call-done = bf16[1536,3072]{1,0:T(8,128)(2,1)} async-done(((bf16[96,3072]{1,0:T(8,128)(2,1)}), bf16[1536,3072]{1,0:T(8,128)(2,1)}) %all-gather.32.cloned.1.call-update) | async-done | bytes 9437200 | tf_op jit(solution)/shard_map/all_gather | solution.py:144
  908.2 62.1 %all-gather.30.cloned.1.call-done = bf16[1536,1536]{1,0:T(8,128)(2,1)} async-done(((bf16[768,1536]{1,0:T(8,128)(2,1)}), bf16[1536,1536]{1,0:T(8,128)(2,1)}) %all-gather.30.cloned.1.call-update) | async-done | bytes 4718608 | tf_op jit(solution)/shard_map/all_gather | solution.py:27
  970.3 21.7 fusion.81
  992.0 42.4 %all-gather.36.cloned.1.call-done = bf16[1536,1536]{1,0:T(8,128)(2,1)} async-done(((bf16[768,1536]{1,0:T(8,128)(2,1)}), bf16[1536,1536]{1,0:T(8,128)(2,1)}) %all-gather.36.cloned.1.call-update) | async-done | bytes 4718608 | tf_op jit(solution)/shard_map/all_gather | solution.py:27
  1034.4 84.4 %all-gather.34.cloned.1.call-done = bf16[3072,1536]{0,1:T(8,128)(2,1)} async-done(((bf16[3072,96]{0,1:T(8,128)(2,1)}), bf16[3072,1536]{0,1:T(8,128)(2,1)}) %all-gather.34.cloned.1.call-update) | async-done | bytes 9437200 | tf_op jit(solution)/shard_map/all_gather | solution.py:145
  1118.7 59.6 %add_convert_fusion = (bf16[1536,3072]{1,0:T(8,128)(2,1)S(1)}, f32[1536,3072]{1,0:T(8,128)}) fusion(f32[1536,3072]{1,0:T(8,128)} %fusion.81, bf16[1536,1536]{1,0:T(8,128)(2,1)} %all-gather.36.cloned.1.call-done, bf16[3072,1536]{0,1:T(8,128)(2,1)} %all-gather.34.cloned.1.call-done), kind=kOutput, calls=%fused_computation.74 | convolution fusion | flops 14835253248 | bytes 61341696 | tf_op jit(solution)/shard_map/td,fd->tf/dot_general | solution.py:193
  1181.8 17.5 fusion.83
  1217.6 17.5 fusion.82
  1235.2 72.8 %reduce-scatter.25.cloned.1.call-done = f32[768,1536]{1,0:T(8,128)} async-done(((f32[1536,1536]{1,0:T(8,128)}), f32[768,1536]{1,0:T(8,128)}) %reduce-scatter.25.cloned.1.call-update) | async-done | bytes 4718608 | tf_op jit(solution)/shard_map/reduce_scatter | solution.py:35
  1313.3 107.6 %reduce-scatter.23.cloned.1.call-done = f32[768,1536]{1,0:T(8,128)} async-done(((f32[1536,1536]{1,0:T(8,128)}), f32[768,1536]{1,0:T(8,128)}) %reduce-scatter.23.cloned.1.call-update) | async-done | bytes 4718608 | tf_op jit(solution)/shard_map/reduce_scatter | solution.py:35
  1436.1 61.9 %all-gather.38.cloned.1.call-done = bf16[1536,1536]{1,0:T(8,128)(2,1)} async-done(((bf16[768,1536]{1,0:T(8,128)(2,1)}), bf16[1536,1536]{1,0:T(8,128)(2,1)}) %all-gather.38.cloned.1.call-update) | async-done | bytes 4718608 | tf_op jit(solution)/shard_map/all_gather | solution.py:27
  1508.1 31.4 while.56
  1552.3 110.7 %reduce-scatter.27.cloned.1.call-done = f32[768,1536]{1,0:T(8,128)} async-done(((f32[1536,1536]{1,0:T(8,128)}), f32[768,1536]{1,0:T(8,128)}) %reduce-scatter.27.cloned.1.call-update) | async-done | bytes 4718608 | tf_op jit(solution)/shard_map/reduce_scatter | solution.py:35
  1680.7 62.7 %all-gather.40.cloned.1.call-done = bf16[1536,1536]{1,0:T(8,128)(2,1)} async-done(((bf16[768,1536]{1,0:T(8,128)(2,1)}), bf16[1536,1536]{1,0:T(8,128)(2,1)}) %all-gather.40.cloned.1.call-update) | async-done | bytes 4718608 | tf_op jit(solution)/shard_map/all_gather | solution.py:27
  1753.5 367.2 %while.57 = (s32[]{:T(128)}, f32[1536,12,64]{0,2,1:T(8,128)}, f32[1536,12,64]{0,2,1:T(8,128)}, bf16[3,512,12,64]{1,3,2,0:T(8,128)(2,1)}, s32[3]{0:T(128)S(1)}, /...) while((s32[]{:T(128)}, f32[1536,12,64]{0,2,1:T(8,128)}, ...), condition=%wide.region_28.29_spmd.clone, body=%wide.region_26.28_spmd.clone.sunk | while | flops 6188427776 | bytes 369013152 | solution.py:114
  1758.1 16.0 fusion.201
  1774.1 19.4 bitcast_add_fusion.5
  1793.5 28.6 multiply_reduce_fusion.14
  1822.1 31.7 multiply_convert_fusion.6
  1879.4 16.0 fusion.201
  1895.4 20.8 bitcast_add_fusion.5
  1916.2 28.6 multiply_reduce_fusion.14
  1944.8 31.7 multiply_convert_fusion.6
  2002.1 16.0 fusion.201
  2018.1 20.7 bitcast_add_fusion.5
  2038.8 28.6 multiply_reduce_fusion.14
  2067.4 31.7 multiply_convert_fusion.6
  2147.8 17.1 convolution_bitcast_fusion.1
  2173.2 14.8 copy.93
  2188.8 86.9 %reduce-scatter.29.cloned.1.call-done = f32[768,1536]{1,0:T(8,128)} async-done(((f32[1536,1536]{1,0:T(8,128)}), f32[768,1536]{1,0:T(8,128)}) %reduce-scatter.29.cloned.1.call-update) | async-done | bytes 4718608 | tf_op jit(solution)/shard_map/reduce_scatter | solution.py:35
  2287.8 21.7 fusion.88
  2309.6 21.5 fusion.89
  2359.3 16.9 fusion.54
  2378.1 85.7 %all-reduce.7.cloned.1.call-done = f32[1536,2,768]{2,1,0:T(2,128)} async-done(((f32[1536,2,768]{2,1,0:T(2,128)}), f32[1536,2,768]{2,1,0:T(2,128)}) %all-reduce.7.cloned.1.call-update) | async-done | bytes 9437200
  2475.4 47.3 %reduce-scatter.45.cloned.1.call-done = f32[96,3]{1,0:T(8,128)} async-done(((f32[1536,3]{1,0:T(8,128)}), f32[96,3]{1,0:T(8,128)}) %reduce-scatter.45.cloned.1.call-update) | async-done | bytes 1168
  2523.6 58.5 %reduce-scatter.43.cloned.1.call-done = f32[96,3]{1,0:T(8,128)} async-done(((f32[1536,3]{1,0:T(8,128)}), f32[96,3]{1,0:T(8,128)}) %reduce-scatter.43.cloned.1.call-update) | async-done | bytes 1168
  2587.3 24.2 all-reduce.5.cloned.1.call-done
  2611.5 198.6 %reduce-scatter.39.cloned.1.call-done = f32[96,3072]{1,0:T(8,128)} async-done(((f32[1536,3072]{1,0:T(8,128)}), f32[96,3072]{1,0:T(8,128)}) %reduce-scatter.39.cloned.1.call-update) | async-done | bytes 1179664 | tf_op jit(solution)/shard_map/reduce_scatter | solution.py:266
  2810.1 197.8 %reduce-scatter.41.cloned.1.call-done = f32[3072,96]{0,1:T(8,128)} async-done(((f32[3072,1536]{0,1:T(8,128)}), f32[3072,96]{0,1:T(8,128)}) %reduce-scatter.41.cloned.1.call-update) | async-done | bytes 1179664 | tf_op jit(solution)/shard_map/reduce_scatter | solution.py:267
  3008.0 77.8 %reduce-scatter.37.cloned.1.call-done = f32[768,96]{0,1:T(8,128)} async-done(((f32[768,1536]{0,1:T(8,128)}), f32[768,96]{0,1:T(8,128)}) %reduce-scatter.37.cloned.1.call-update) | async-done | bytes 294928 | tf_op jit(solution)/shard_map/reduce_scatter | solution.py:265
  3085.8 78.6 %reduce-scatter.35.cloned.1.call-done = f32[96,768]{1,0:T(8,128)} async-done(((f32[1536,768]{1,0:T(8,128)}), f32[96,768]{1,0:T(8,128)}) %reduce-scatter.35.cloned.1.call-update) | async-done | bytes 294928 | tf_op jit(solution)/shard_map/reduce_scatter | solution.py:263
  3164.4 79.2 %reduce-scatter.33.cloned.1.call-done = f32[768,96]{0,1:T(8,128)} async-done(((f32[768,1536]{0,1:T(8,128)}), f32[768,96]{0,1:T(8,128)}) %reduce-scatter.33.cloned.1.call-update) | async-done | bytes 294928 | tf_op jit(solution)/shard_map/reduce_scatter | solution.py:262
  3243.6 150.6 %reduce-scatter.31.cloned.1.call-done = f32[96,3,768]{2,0,1:T(8,128)} async-done(((f32[1536,3,768]{2,0,1:T(8,128)}), f32[96,3,768]{2,0,1:T(8,128)}) %reduce-scatter.31.cloned.1.call-update) | async-done | bytes 884752 | tf_op jit(solution)/shard_map/reduce_scatter | solution.py:261
  (436 shorter events, 397.0 us)
Async XLA Ops:
  7.2 114.7 %all-gather.16.cloned.1.call-start = ((), (), s32[]{:S(2)}) async-start(), calls=%async_computation.14 | async-start | bytes 7077888 | tf_op jit(solution)/shard_map/all_gather | solution.py:27
  11.2 50.1 %copy-start.43 = (f32[768]{0:T(1024)}, f32[768]{0:T(1024)S(1)}, u32[]{:S(2)}) copy-start(f32[768]{0:T(1024)S(1)} %broadcast_multiply_fusion.2) | copy-start | bytes 9220
  14.2 23.0 copy-start.53
  14.2 47.2 %copy-start.49 = (f32[768]{0:T(1024)}, f32[768]{0:T(1024)S(1)}, u32[]{:S(2)}) copy-start(f32[768]{0:T(1024)S(1)} %fusion.62) | copy-start | bytes 9220
  61.4 130.0 %all-gather.18.cloned.1.call-start = ((), (), s32[]{:S(2)}) async-start(), calls=%async_computation.15 | async-start | bytes 7520256 | tf_op jit(solution)/shard_map/all_gather | solution.py:139
  62.3 315.1 %all-gather.20.cloned.1.call-start = ((), (), s32[]{:S(2)}) async-start(), calls=%async_computation.16 | async-start | bytes 2506752 | tf_op jit(solution)/shard_map/all_gather | solution.py:140
  63.0 433.3 %reduce-scatter.19.cloned.1.call-start = ((), (), s32[]{:S(2)}) async-start(), calls=%async_computation.17 | async-start | bytes 14155776 | tf_op jit(solution)/shard_map/reduce_scatter | solution.py:35
  230.1 17.5 copy-start.5
  283.2 17.4 copy-start.5
  387.4 165.4 %all-gather.26.cloned.1.call-start = ((), (), s32[]{:S(2)}) async-start(), calls=%async_computation.20 | async-start | bytes 5013504 | tf_op jit(solution)/shard_map/all_gather | solution.py:142
  389.2 207.2 %all-gather.24.cloned.1.call-start = ((), (), s32[]{:S(2)}) async-start(), calls=%async_computation.19 | async-start | bytes 2506752 | tf_op jit(solution)/shard_map/all_gather | solution.py:141
  389.9 269.4 %all-gather.22.cloned.1.call-start = ((), (), s32[]{:S(2)}) async-start(), calls=%async_computation.18 | async-start | bytes 7077888 | tf_op jit(solution)/shard_map/all_gather | solution.py:27
  502.9 49.9 %copy-start.24 = (f32[1,64,1536]{2,1,0:T(8,128)S(1)}, f32[1,64,1536]{2,1,0:T(8,128)}, u32[]{:S(2)}) copy-start(f32[1,64,1536]{2,1,0:T(8,128)} %param.21) | copy-start | bytes 1179652
  505.1 200.0 %all-gather.28.cloned.1.call-start = ((), (), s32[]{:S(2)}) async-start(), calls=%async_computation.21 | async-start | bytes 2506752 | tf_op jit(solution)/shard_map/all_gather | solution.py:143
  505.9 318.1 %reduce-scatter.21.cloned.1.call-start = ((), (), s32[]{:S(2)}) async-start(), calls=%async_computation.22 | async-start | bytes 14155776 | tf_op jit(solution)/shard_map/reduce_scatter | solution.py:35
  556.2 40.1 %copy-start.18 = (bf16[64,12,64]{2,1,0:T(8,128)(2,1)}, bf16[64,12,64]{2,1,0:T(8,128)(2,1)S(1)}, u32[]{:S(2)}) copy-start(bf16[64,12,64]{2,1,0:T(8,128)(2,1)S(1)} %reshape_squeeze.19) | copy-start | bytes 294916
  556.7 39.7 %copy-start.20 = (bf16[64,12,64]{2,1,0:T(8,128)(2,1)}, bf16[64,12,64]{2,1,0:T(8,128)(2,1)S(1)}, u32[]{:S(2)}) copy-start(bf16[64,12,64]{2,1,0:T(8,128)(2,1)S(1)} %reshape_squeeze.18) | copy-start | bytes 294916
  715.1 193.2 %all-gather.32.cloned.1.call-start = ((), (), s32[]{:S(2)}) async-start(), calls=%async_computation.24 | async-start | bytes 10027008 | tf_op jit(solution)/shard_map/all_gather | solution.py:144
  717.2 253.1 %all-gather.30.cloned.1.call-start = ((), (), s32[]{:S(2)}) async-start(), calls=%async_computation.23 | async-start | bytes 7077888 | tf_op jit(solution)/shard_map/all_gather | solution.py:27
  832.8 201.5 %all-gather.36.cloned.1.call-start = ((), (), s32[]{:S(2)}) async-start(), calls=%async_computation.27 | async-start | bytes 7077888 | tf_op jit(solution)/shard_map/all_gather | solution.py:27
  837.3 281.5 %all-gather.34.cloned.1.call-start = ((), (), s32[]{:S(2)}) async-start(), calls=%async_computation.25 | async-start | bytes 10027008 | tf_op jit(solution)/shard_map/all_gather | solution.py:145
  838.2 469.8 %reduce-scatter.25.cloned.1.call-start = ((), (), s32[]{:S(2)}) async-start(), calls=%async_computation.28 | async-start | bytes 14155776 | tf_op jit(solution)/shard_map/reduce_scatter | solution.py:35
  1118.7 63.1 %copy-start.65 = (bf16[1536,3072]{1,0:T(8,128)(2,1)S(1)}, bf16[1536,3072]{1,0:T(8,128)(2,1)}, u32[]{:S(2)}) copy-start(bf16[1536,3072]{1,0:T(8,128)(2,1)} %all-gather.32.cloned.1.call-done) | copy-start | bytes 28311556
  1199.4 18.3 slice-start.6
  1199.4 221.5 %reduce-scatter.23.cloned.1.call-start = ((), (), s32[]{:S(2)}) async-start(), calls=%async_computation.26 | async-start | bytes 14155776 | tf_op jit(solution)/shard_map/reduce_scatter | solution.py:35
  1199.5 18.2 slice-start.7
  1199.5 18.2 slice-start.8
  1235.1 72.9 %copy-start.40 = (f32[1536]{0:T(1024)S(1)}, f32[1536]{0:T(1024)}, u32[]{:S(2)}) copy-start(f32[1536]{0:T(1024)} %get-tuple-element.373) | copy-start | bytes 18436
  1235.1 72.9 %copy-start.42 = (f32[768]{0:T(1024)S(1)}, f32[768]{0:T(1024)}, u32[]{:S(2)}) copy-start(f32[768]{0:T(1024)} %copy-done.41) | copy-start | bytes 9220
  1235.1 72.9 %copy-start.48 = (f32[768]{0:T(1024)S(1)}, f32[768]{0:T(1024)}, u32[]{:S(2)}) copy-start(f32[768]{0:T(1024)} %copy-done.47) | copy-start | bytes 9220
  1235.1 78.1 %copy-start.58 = (f32[768]{0:T(1024)S(1)}, f32[768]{0:T(1024)}, u32[]{:S(2)}) copy-start(f32[768]{0:T(1024)} %copy-done.57) | copy-start | bytes 9220
  1235.1 262.8 %all-gather.38.cloned.1.call-start = ((), (), s32[]{:S(2)}) async-start(), calls=%async_computation.29 | async-start | bytes 7077888 | tf_op jit(solution)/shard_map/all_gather | solution.py:27
  1435.2 227.8 %reduce-scatter.27.cloned.1.call-start = ((), (), s32[]{:S(2)}) async-start(), calls=%async_computation.30 | async-start | bytes 14155776 | tf_op jit(solution)/shard_map/reduce_scatter | solution.py:35
  1436.1 72.0 %copy-start.7 = (bf16[1536,12,64]{0,2,1:T(8,128)(2,1)S(1)}, bf16[1536,12,64]{0,2,1:T(8,128)(2,1)}, u32[]{:S(2)}) copy-start(bf16[1536,12,64]{0,2,1:T(8,128)(2,1)} %copy-done.6) | copy-start | bytes 7077892
  1552.2 110.8 %copy-start.38 = (f32[1536]{0:T(1024)S(1)}, f32[1536]{0:T(1024)}, u32[]{:S(2)}) copy-start(f32[1536]{0:T(1024)} %get-tuple-element.374) | copy-start | bytes 18436
  1552.2 110.8 %copy-start.46 = (f32[768]{0:T(1024)S(1)}, f32[768]{0:T(1024)}, u32[]{:S(2)}) copy-start(f32[768]{0:T(1024)} %copy-done.45) | copy-start | bytes 9220
  1552.2 110.8 %copy-start.52 = (f32[768]{0:T(1024)S(1)}, f32[768]{0:T(1024)}, u32[]{:S(2)}) copy-start(f32[768]{0:T(1024)} %copy-done.51) | copy-start | bytes 9220
  1552.2 116.2 %copy-start.56 = (f32[768]{0:T(1024)S(1)}, f32[768]{0:T(1024)}, u32[]{:S(2)}) copy-start(f32[768]{0:T(1024)} %copy-done.55) | copy-start | bytes 9220
  1552.2 191.2 %all-gather.40.cloned.1.call-start = ((), (), s32[]{:S(2)}) async-start(), calls=%async_computation.31 | async-start | bytes 7077888 | tf_op jit(solution)/shard_map/all_gather | solution.py:27
  1680.6 595.1 %reduce-scatter.29.cloned.1.call-start = ((), (), s32[]{:S(2)}) async-start(), calls=%async_computation.32 | async-start | bytes 14155776 | tf_op jit(solution)/shard_map/reduce_scatter | solution.py:35
  1680.7 72.8 %copy-start.1 = (bf16[1536,12,64]{0,2,1:T(8,128)(2,1)S(1)}, bf16[1536,12,64]{0,2,1:T(8,128)(2,1)}, u32[]{:S(2)}) copy-start(bf16[1536,12,64]{0,2,1:T(8,128)(2,1)} %copy-done) | copy-start | bytes 7077892
  1793.5 70.0 %slice-start = ((s8[4718592]{0:T(1024)(128)(4,1)}), s8[4194304]{0:T(1024)(128)(4,1)S(1)}, s32[]{:S(2)}) async-start(s8[4718592]{0:T(1024)(128)(4,1)} %bitcast.220), calls=%async_computation.43 | async-start | bytes 8388608 | tf_op jit(solution)/shard_map/while
  1822.1 31.7 copy-start.13
  1822.1 41.5 %slice-start.1 = ((s8[4718592]{0:T(1024)(128)(4,1)}), s8[524288]{0:T(1024)(128)(4,1)S(1)}, s32[]{:S(2)}) async-start(s8[4718592]{0:T(1024)(128)(4,1)} %bitcast.220), calls=%async_computation.44 | async-start | bytes 1048576 | tf_op jit(solution)/shard_map/while
  1916.2 70.0 %slice-start = ((s8[4718592]{0:T(1024)(128)(4,1)}), s8[4194304]{0:T(1024)(128)(4,1)S(1)}, s32[]{:S(2)}) async-start(s8[4718592]{0:T(1024)(128)(4,1)} %bitcast.220), calls=%async_computation.43 | async-start | bytes 8388608 | tf_op jit(solution)/shard_map/while
  1944.8 31.7 copy-start.13
  1944.8 41.5 %slice-start.1 = ((s8[4718592]{0:T(1024)(128)(4,1)}), s8[524288]{0:T(1024)(128)(4,1)S(1)}, s32[]{:S(2)}) async-start(s8[4718592]{0:T(1024)(128)(4,1)} %bitcast.220), calls=%async_computation.44 | async-start | bytes 1048576 | tf_op jit(solution)/shard_map/while
  2038.8 70.0 %slice-start = ((s8[4718592]{0:T(1024)(128)(4,1)}), s8[4194304]{0:T(1024)(128)(4,1)S(1)}, s32[]{:S(2)}) async-start(s8[4718592]{0:T(1024)(128)(4,1)} %bitcast.220), calls=%async_computation.43 | async-start | bytes 8388608 | tf_op jit(solution)/shard_map/while
  2067.4 31.7 copy-start.13
  2067.4 41.5 %slice-start.1 = ((s8[4718592]{0:T(1024)(128)(4,1)}), s8[524288]{0:T(1024)(128)(4,1)S(1)}, s32[]{:S(2)}) async-start(s8[4718592]{0:T(1024)(128)(4,1)} %bitcast.220), calls=%async_computation.44 | async-start | bytes 1048576 | tf_op jit(solution)/shard_map/while
  2165.0 298.9 %all-reduce.7.cloned.1.call-start = ((), (), s32[]{:S(2)}) async-start(), calls=%async_computation.42 | async-start | bytes 18874368
  2188.1 87.7 %copy-start.36 = (f32[1536]{0:T(1024)S(1)}, f32[1536]{0:T(1024)}, u32[]{:S(2)}) copy-start(f32[1536]{0:T(1024)} %copy-done.35) | copy-start | bytes 18436
  2188.1 87.7 %copy-start.44 = (f32[768]{0:T(1024)S(1)}, f32[768]{0:T(1024)}, u32[]{:S(2)}) copy-start(f32[768]{0:T(1024)} %copy-done.43) | copy-start | bytes 9220
  2188.1 87.7 %copy-start.50 = (f32[768]{0:T(1024)S(1)}, f32[768]{0:T(1024)}, u32[]{:S(2)}) copy-start(f32[768]{0:T(1024)} %copy-done.49) | copy-start | bytes 9220
  2188.1 334.6 %reduce-scatter.45.cloned.1.call-start = ((), (), s32[]{:S(2)}) async-start(), calls=%async_computation.41 | async-start | bytes 835584
  2281.7 300.3 %reduce-scatter.43.cloned.1.call-start = ((), (), s32[]{:S(2)}) async-start(), calls=%async_computation.40 | async-start | bytes 835584
  2283.0 328.5 %all-reduce.5.cloned.1.call-start = ((), (), s32[]{:S(2)}) async-start(), calls=%async_computation.33 | async-start | bytes 786432 | tf_op jit(solution)/shard_map/psum | solution.py:255
  2287.8 522.3 %reduce-scatter.39.cloned.1.call-start = ((), (), s32[]{:S(2)}) async-start(), calls=%async_computation.38 | async-start | bytes 20054016 | tf_op jit(solution)/shard_map/reduce_scatter | solution.py:266
  2309.6 698.4 %reduce-scatter.41.cloned.1.call-start = ((), (), s32[]{:S(2)}) async-start(), calls=%async_computation.39 | async-start | bytes 20054016 | tf_op jit(solution)/shard_map/reduce_scatter | solution.py:267
  2331.1 754.7 %reduce-scatter.37.cloned.1.call-start = ((), (), s32[]{:S(2)}) async-start(), calls=%async_computation.37 | async-start | bytes 5013504 | tf_op jit(solution)/shard_map/reduce_scatter | solution.py:265
  2340.6 823.8 %reduce-scatter.35.cloned.1.call-start = ((), (), s32[]{:S(2)}) async-start(), calls=%async_computation.36 | async-start | bytes 5013504 | tf_op jit(solution)/shard_map/reduce_scatter | solution.py:263
  2349.9 893.7 %reduce-scatter.33.cloned.1.call-start = ((), (), s32[]{:S(2)}) async-start(), calls=%async_computation.35 | async-start | bytes 5013504 | tf_op jit(solution)/shard_map/reduce_scatter | solution.py:262
  2359.3 1034.9 %reduce-scatter.31.cloned.1.call-start = ((), (), s32[]{:S(2)}) async-start(), calls=%async_computation.34 | async-start | bytes 15040512 | tf_op jit(solution)/shard_map/reduce_scatter | solution.py:261
  2376.2 89.6 %copy-start.54 = (f32[768]{0:T(1024)S(1)}, f32[768]{0:T(1024)}, u32[]{:S(2)}) copy-start(f32[768]{0:T(1024)} %copy-done.53) | copy-start | bytes 9220
  (59 other events, 224.1 us)
Sparse Core Ops, SparseCore 0:
  61.5 60.3 all-gather.15
  124.8 66.6 all-gather.17
  194.3 41.0 all-gather.19
  387.5 108.8 reduce-scatter.18
  499.0 53.7 all-gather.25
  555.5 40.8 all-gather.23
  598.5 60.7 all-gather.21
  662.2 42.9 all-gather.27
  715.2 108.7 reduce-scatter.20
  826.7 81.4 all-gather.31
  909.8 60.4 all-gather.29
  971.7 62.6 all-gather.35
  1037.2 81.4 all-gather.33
  1199.5 108.4 reduce-scatter.24
  1310.2 110.6 reduce-scatter.22
  1435.3 62.6 all-gather.37
  1552.4 110.6 reduce-scatter.26
  1680.8 62.6 all-gather.39
  2165.1 110.6 reduce-scatter.28
  2279.3 184.5 all-reduce.6
  2467.4 55.2 reduce-scatter.44
  2526.3 55.7 reduce-scatter.42
  2584.9 26.5 all-reduce.4
  2616.1 194.0 reduce-scatter.38
  2814.8 193.1 reduce-scatter.40
  3012.3 73.4 reduce-scatter.36
  3090.0 74.3 reduce-scatter.34
  3168.8 74.7 reduce-scatter.32
  3248.4 145.8 reduce-scatter.30
where the time goes:
time: 3410 us; the launch traced here: 3400 us
  waiting for transfers between devices  2270 us (67%)
  matrix products  671 us (20%)
  other arithmetic  257 us (8%)
  local copies, waits for them, and re-layouts  119 us (3%)
  blocking collectives  44.8 us (1%)
    reduce_scatter x6, waiting for transfers between devices, project_rows(): lax.psum_scatter(jnp.einsum(pattern, operand, weight, preferred_element_t...  591 us
    all_gather x6, waiting for transfers between devices, gather_rows(): return lax.all_gather(local_rows, 'tensor', axis=0, tiled=True)  351 us
    reduce_scatter x1, waiting for transfers between devices, on_device(): lax.psum_scatter(up_grad, 'dp', scatter_dimension=0, tiled=True)  199 us
    reduce_scatter x1, waiting for transfers between devices, on_device(): lax.psum_scatter(down_grad, 'dp', scatter_dimension=1, tiled=True)  198 us
    unnamed x32, waiting for transfers between devices  192 us
    reduce_scatter x1, waiting for transfers between devices, on_device(): lax.psum_scatter(qkv_weight_grad, 'dp', scatter_dimension=0, tiled=True)  151 us
    dot_general x12, matrix products, score_block(): jnp.einsum('bhe,khe->hbk', query_block, keys, preferred_element_type=jnp....  102 us
    convert_element_type x6, other arithmetic, one_block(): score_grads = (probs * (prob_grads - centre)).astype(jnp.bfloat16)  96.4 us
  transfers between devices with their start and end apart: 29, of which 28 were waited for; matrix products, arithmetic and copies ran while one was open for 13% of the time, Pallas kernels for 0%

commit v1 on v0

--- a/solution.py
+++ b/solution.py
@@ -1,8 +1,12 @@
+import functools
 import math
 
 import jax
 import jax.numpy as jnp
 from jax import lax
+from jax.experimental import pallas as pl
+from jax.experimental.pallas import tpu as pltpu
+from jax.sharding import Mesh
 from jax.sharding import PartitionSpec as P
 
 HEAD_DIM = 64
@@ -293,38 +297,430 @@
     )
 
 
+PAIR = 2 * HEAD_DIM
+ROWS_STEP = 512
+LOG2E = 1.4426950408889634
+VMEM_BYTES = 60 * 1024 * 1024
+
+
+def dot_last(left, right):
+    return lax.dot_general(left, right, (((1,), (1,)), ((), ())), preferred_element_type=jnp.float32)
+
+
+def dot_first(left, right):
+    return lax.dot_general(left, right, (((0,), (0,)), ((), ())), preferred_element_type=jnp.float32)
+
+
+def key_spans(step, block, key_count, causal):
+    if not causal:
+        return [(0, key_count, False)]
+    spans = [(0, step * block, False)] if step else []
+    return spans + [(step * block, block, True)]
+
+
+def causal_keep(block):
+    key_pos = lax.broadcasted_iota(jnp.int32, (block, block), 0)
+    query_pos = lax.broadcasted_iota(jnp.int32, (block, block), 1)
+    return key_pos <= query_pos
+
+
+def head_lanes(head):
+    lanes = lax.broadcasted_iota(jnp.int32, (1, PAIR), 1)
+    return (lanes >= HEAD_DIM) == (head == 1)
+
+
+def attend_kernel(causal, block, q_ref, k_ref, v_ref, out_ref, log_ref, total_ref):
+    length, key_count = q_ref.shape[0], k_ref.shape[0]
+    scale = LOG2E / math.sqrt(HEAD_DIM)
+
+    def one_head(head, carry):
+        keep = head_lanes(head)
+        mask = keep.astype(jnp.float32).astype(jnp.bfloat16)
+        for step in range(length // block):
+            rows = pl.ds(step * block, block)
+            queries = q_ref[rows, :] * mask
+            scores = []
+            for start, count, diagonal in key_spans(step, block, key_count, causal):
+                part = dot_last(k_ref[pl.ds(start, count), :], queries)
+                if diagonal:
+                    part = jnp.where(causal_keep(block), part, MASKED)
+                scores.append(part)
+            highest = jnp.max(scores[0], axis=0, keepdims=True)
+            for part in scores[1:]:
+                highest = jnp.maximum(highest, jnp.max(part, axis=0, keepdims=True))
+            total, mixed = None, None
+            for part, (start, count, _) in zip(scores, key_spans(step, block, key_count, causal)):
+                raised = jnp.exp2((part - highest) * scale)
+                summed = jnp.sum(raised, axis=0, keepdims=True)
+                product = dot_first(v_ref[pl.ds(start, count), :], raised.astype(jnp.bfloat16))
+                total = summed if total is None else total + summed
+                mixed = product if mixed is None else mixed + product
+            total_ref[rows, :] = jnp.where(keep, (mixed / total).T, total_ref[rows, :])
+            log_ref[0, pl.ds(head, 1), rows] = highest * scale + jnp.log2(total)
+        return carry
+
+    lax.fori_loop(0, 2, one_head, 0)
+    out_ref[...] = total_ref[...].astype(jnp.bfloat16)
+
+
+def attend_back_body(
+    causal, block, q_ref, k_ref, v_ref, grad_ref, log_ref, dq_ref, dk_ref, dv_ref
+):
+    length, key_count = q_ref.shape[0], k_ref.shape[0]
+    scale = 1.0 / math.sqrt(HEAD_DIM)
+    dk_ref[...] = jnp.zeros_like(dk_ref)
+    dv_ref[...] = jnp.zeros_like(dv_ref)
+
+    def one_head(head, carry):
+        keep = head_lanes(head)
+        mask = keep.astype(jnp.float32).astype(jnp.bfloat16)
+        for step in range(length // block):
+            rows = pl.ds(step * block, block)
+            queries = q_ref[rows, :] * mask
+            grads = grad_ref[rows, :] * mask
+            logs = log_ref[0, pl.ds(head, 1), rows]
+            spans = key_spans(step, block, key_count, causal)
+            held, centre = [], None
+            for start, count, diagonal in spans:
+                keys = pl.ds(start, count)
+                probs = jnp.exp2(dot_last(k_ref[keys, :], queries) * (scale * LOG2E) - logs)
+                if diagonal:
+                    probs = jnp.where(causal_keep(block), probs, 0.0)
+                dv_ref[keys, :] += jnp.dot(
+                    probs.astype(jnp.bfloat16), grads, preferred_element_type=jnp.float32
+                )
+                prob_grads = dot_last(v_ref[keys, :], grads)
+                summed = jnp.sum(probs * prob_grads, axis=0, keepdims=True)
+                centre = summed if centre is None else centre + summed
+                held.append((probs, prob_grads))
+            mixed = None
+            for (probs, prob_grads), (start, count, _) in zip(held, spans):
+                keys = pl.ds(start, count)
+                score_grads = (probs * (prob_grads - centre)).astype(jnp.bfloat16)
+                dk_ref[keys, :] += jnp.dot(
+                    score_grads, queries, preferred_element_type=jnp.float32
+                )
+                product = dot_first(k_ref[keys, :], score_grads)
+                mixed = product if mixed is None else mixed + product
+            dq_ref[rows, :] = jnp.where(keep, mixed.T, dq_ref[rows, :])
+        return carry
+
+    lax.fori_loop(0, 2, one_head, 0)
+
+
+def self_back_kernel(
+    block, q_ref, k_ref, v_ref, grad_ref, log_ref, out_ref, dq_ref, dk_ref, dv_ref
+):
+    scale = 1.0 / math.sqrt(HEAD_DIM)
+    part = pl.program_id(1)
+
+    @pl.when(part == 0)
+    def _():
+        attend_back_body(
+            True, block, q_ref, k_ref, v_ref, grad_ref, log_ref, dq_ref, dk_ref, dv_ref
+        )
+        out_ref[...] = (dq_ref[...] * scale).astype(jnp.bfloat16)
+
+    @pl.when(part == 1)
+    def _():
+        out_ref[...] = (dk_ref[...] * scale).astype(jnp.bfloat16)
+
+    @pl.when(part == 2)
+    def _():
+        out_ref[...] = dv_ref[...].astype(jnp.bfloat16)
+
+
+def cross_back_kernel(
+    block,
+    q_ref,
+    k_ref,
+    v_ref,
+    grad_ref,
+    log_ref,
+    query_ref,
+    key_ref,
+    value_ref,
+    dq_ref,
+    dk_ref,
+    dv_ref,
+):
+    scale = 1.0 / math.sqrt(HEAD_DIM)
+    attend_back_body(
+        False, block, q_ref, k_ref, v_ref, grad_ref, log_ref, dq_ref, dk_ref, dv_ref
+    )
+    query_ref[...] = (dq_ref[...] * scale).astype(jnp.bfloat16)
+    key_ref[...] = (dk_ref[...] * scale).astype(jnp.bfloat16)
+    value_ref[...] = dv_ref[...].astype(jnp.bfloat16)
+
+
+def column_spec(rows, first):
+    return pl.BlockSpec((rows, PAIR), lambda pair, *rest: (0, first + pair))
+
+
+def log_spec(rows):
+    return pl.BlockSpec((1, 2, rows), lambda pair, *rest: (pair, 0, 0))
+
+
+def attention_cost(length, key_count, lanes, products):
+    return pl.CostEstimate(
+        flops=2 * products * length * key_count * lanes,
+        transcendentals=length * key_count * lanes // HEAD_DIM,
+        bytes_accessed=2 * products * (length + key_count) * lanes,
+    )
+
+
+def fused_attend(queries, keys, first_key, first_value, lanes, causal):
+    length, key_count = queries.shape[0], keys.shape[0]
+    pairs = lanes // PAIR
+    block = min(ROWS_STEP, length)
+    return pl.pallas_call(
+        functools.partial(attend_kernel, causal, block),
+        grid=(pairs,),
+        in_specs=[
+            column_spec(length, 0),
+            column_spec(key_count, first_key),
+            column_spec(key_count, first_value),
+        ],
+        out_specs=[column_spec(length, 0), log_spec(length)],
+        out_shape=[
+            jax.ShapeDtypeStruct((length, lanes), jnp.bfloat16),
+            jax.ShapeDtypeStruct((pairs, 2, length), jnp.float32),
+        ],
+        scratch_shapes=[pltpu.VMEM((length, PAIR), jnp.float32)],
+        compiler_params=pltpu.CompilerParams(vmem_limit_bytes=VMEM_BYTES),
+        cost_estimate=attention_cost(length, key_count, lanes, 2),
+        name="attend_self" if causal else "attend_cross",
+    )(queries, keys, keys)
+
+
+def accumulators(length, key_count):
+    return [
+        pltpu.VMEM((length, PAIR), jnp.float32),
+        pltpu.VMEM((key_count, PAIR), jnp.float32),
+        pltpu.VMEM((key_count, PAIR), jnp.float32),
+    ]
+
+
+def fused_self_back(triple, logs, grads):
+    length, lanes = grads.shape
+    pairs = lanes // PAIR
+    return pl.pallas_call(
+        functools.partial(self_back_kernel, min(ROWS_STEP, length)),
+        grid=(pairs, 3),
+        in_specs=[
+            column_spec(length, 0),
+            column_spec(length, pairs),
+            column_spec(length, 2 * pairs),
+            column_spec(length, 0),
+            log_spec(length),
+        ],
+        out_specs=pl.BlockSpec((length, PAIR), lambda pair, part: (0, part * pairs + pair)),
+        out_shape=jax.ShapeDtypeStruct((length, 3 * lanes), jnp.bfloat16),
+        scratch_shapes=accumulators(length, length),
+        compiler_params=pltpu.CompilerParams(vmem_limit_bytes=VMEM_BYTES),
+        cost_estimate=attention_cost(length, length, lanes, 5),
+        name="attend_self_back",
+    )(triple, triple, triple, grads, logs)
+
+
+def fused_cross_back(queries, text_pair, logs, grads):
+    length, lanes = grads.shape
+    key_count = text_pair.shape[0]
+    pairs = lanes // PAIR
+    return pl.pallas_call(
+        functools.partial(cross_back_kernel, min(ROWS_STEP, length)),
+        grid=(pairs,),
+        in_specs=[
+            column_spec(length, 0),
+            column_spec(key_count, 0),
+            column_spec(key_count, pairs),
+            column_spec(length, 0),
+            log_spec(length),
+        ],
+        out_specs=[column_spec(length, 0), column_spec(key_count, 0), column_spec(key_count, 0)],
+        out_shape=[
+            jax.ShapeDtypeStruct((length, lanes), jnp.bfloat16),
+            jax.ShapeDtypeStruct((key_count, lanes), jnp.bfloat16),
+            jax.ShapeDtypeStruct((key_count, lanes), jnp.bfloat16),
+        ],
+        scratch_shapes=accumulators(length, key_count),
+        compiler_params=pltpu.CompilerParams(vmem_limit_bytes=VMEM_BYTES),
+        cost_estimate=attention_cost(length, key_count, lanes, 5),
+        name="attend_cross_back",
+    )(queries, text_pair, text_pair, grads, logs)
+
+
+SPREAD = ("site", "y")
+
+
+def low(values):
+    return values.astype(jnp.bfloat16)
+
+
+def trade_corners(values):
+    return lax.ppermute(values, ("core", "y"), [(0, 0), (1, 2), (2, 1), (3, 3)])
+
+
+def to_mate(values):
+    return lax.ppermute(values, "core", [(0, 1), (1, 0)])
+
+
+def gather_pair(local_rows):
+    other = to_mate(local_rows)
+    first = lax.axis_index("core") == 0
+    return jnp.concatenate(
+        [jnp.where(first, local_rows, other), jnp.where(first, other, local_rows)], axis=0
+    )
+
+
+def scatter_pair(operand, product):
+    rows = operand.shape[0] // 2
+    core = lax.axis_index("core")
+    theirs = low(product(lax.dynamic_slice_in_dim(operand, (1 - core) * rows, rows, 0)))
+    received = to_mate(theirs)
+    mine = product(lax.dynamic_slice_in_dim(operand, core * rows, rows, 0))
+    return mine + received.astype(jnp.float32)
+
+
+def fetch(shard):
+    return lax.all_gather(trade_corners(shard), SPREAD, axis=0, tiled=True)
+
+
+def share_grad(grad):
+    summed = lax.psum_scatter(low(grad), SPREAD, scatter_dimension=0, tiled=True)
+    return trade_corners(summed).astype(jnp.float32)
+
+
+def on_pair(
+    states,
+    text_states,
+    norm_gains,
+    norm_biases,
+    self_qkv,
+    self_out,
+    cross_query,
+    cross_kv,
+    cross_out,
+    mlp_up,
+    mlp_down,
+    out_grad,
+):
+    depth, _, lanes = self_qkv.shape
+    pairs = lanes // PAIR
+    f32 = jnp.float32
+    norms = lax.all_gather(
+        low(jnp.concatenate([norm_gains, norm_biases], axis=0)), ("site", "core"), axis=1, tiled=True
+    ).astype(f32)
+    gains, biases = norms[:3], norms[3:]
+    w_qkv = fetch(low(self_qkv).reshape(depth, 3 * lanes))
+    w_self_out = fetch(low(self_out).T)
+    w_kv = fetch(low(cross_kv).reshape(depth, 2 * lanes))
+    w_query = fetch(low(cross_query))
+    w_cross_out = fetch(low(cross_out).T)
+    w_up = fetch(low(mlp_up))
+    w_down = fetch(low(mlp_down).T)
+    rows = trade_corners(states)
+    text_low = trade_corners(low(text_states[0]))
+    grad_rows = trade_corners(low(out_grad))
+
+    def norm_back(values, which, grads):
+        _, pull = jax.vjp(normalize, values, gains[which], biases[which])
+        return pull(grads)
+
+    def dot(left, right):
+        return jnp.dot(left, right, preferred_element_type=f32)
+
+    normed_one = gather_pair(low(normalize(rows, gains[0], biases[0])))
+    triple = low(dot(normed_one, w_qkv))
+    self_mixed, self_logs = fused_attend(triple, triple, pairs, 2 * pairs, lanes, True)
+    after_self = rows + scatter_pair(self_mixed, lambda part: dot_last(part, w_self_out))
+    normed_two = gather_pair(low(normalize(after_self, gains[1], biases[1])))
+    queries = low(dot(normed_two, w_query))
+    text_pair = low(dot(text_low, w_kv))
+    cross_mixed, cross_logs = fused_attend(queries, text_pair, 0, pairs, lanes, False)
+    after_cross = after_self + scatter_pair(cross_mixed, lambda part: dot_last(part, w_cross_out))
+    normed_three = gather_pair(low(normalize(after_cross, gains[2], biases[2])))
+    hidden_pre = dot(normed_three, w_up)
+    hidden = low(activate(hidden_pre))
+    layer_out = trade_corners(
+        after_cross + scatter_pair(hidden, lambda part: dot_last(part, w_down))
+    )
+    branch_grads = gather_pair(grad_rows)
+    down_grad = share_grad(dot_first(branch_grads, hidden)).T
+    hidden_grad = dot(branch_grads, w_down)
+    _, pull_act = jax.vjp(activate, hidden_pre)
+    pre_grad = low(pull_act(hidden_grad)[0])
+    up_grad = share_grad(dot_first(normed_three, pre_grad))
+    back_three = scatter_pair(pre_grad, lambda part: dot_last(part, w_up))
+    rows_three, gain_three, shift_three = norm_back(after_cross, 2, back_three)
+    cross_rows_grad = grad_rows.astype(f32) + rows_three
+    cross_grads = gather_pair(low(cross_rows_grad))
+    cross_out_grad = share_grad(dot_first(cross_grads, cross_mixed)).T
+    cross_mixed_grad = low(dot(cross_grads, w_cross_out))
+    query_grad, key_grad, value_grad = fused_cross_back(
+        queries, text_pair, cross_logs, cross_mixed_grad
+    )
+    pair_grad = jnp.concatenate([key_grad, value_grad], axis=1)
+    query_weight_grad = share_grad(dot_first(normed_two, query_grad))
+    kv_weight_grad = share_grad(dot_first(text_low, pair_grad)).reshape(depth, 2, lanes)
+    text_part = dot_last(pair_grad, w_kv)
+    text_grad = trade_corners(text_part + to_mate(text_part))
+    back_two = scatter_pair(query_grad, lambda part: dot_last(part, w_query))
+    rows_two, gain_two, shift_two = norm_back(after_self, 1, back_two)
+    self_rows_grad = cross_rows_grad + rows_two
+    self_grads = gather_pair(low(self_rows_grad))
+    self_out_grad = share_grad(dot_first(self_grads, self_mixed)).T
+    self_mixed_grad = low(dot(self_grads, w_self_out))
+    triple_grad = fused_self_back(triple, self_logs, self_mixed_grad)
+    qkv_grad = share_grad(dot_first(normed_one, triple_grad)).reshape(depth, 3, lanes)
+    back_one = scatter_pair(triple_grad, lambda part: dot_last(part, w_qkv))
+    rows_one, gain_one, shift_one = norm_back(rows, 0, back_one)
+    states_grad = trade_corners(self_rows_grad + rows_one)
+    norm_parts = jnp.stack([gain_one, gain_two, gain_three, shift_one, shift_two, shift_three])
+    norm_total = lax.psum(norm_parts, ("site", "core", "y"))
+    width = norm_gains.shape[1]
+    place = lax.axis_index("site") * 2 + lax.axis_index("core")
+    norm_own = lax.dynamic_slice_in_dim(norm_total, place * width, width, 1)
+    return (
+        layer_out,
+        states_grad,
+        text_grad[None],
+        norm_own[:3],
+        norm_own[3:],
+        qkv_grad,
+        self_out_grad,
+        query_weight_grad,
+        kv_weight_grad,
+        cross_out_grad,
+        up_grad,
+        down_grad,
+    )
+
+
+def placements(dp, tensor):
+    both = (*dp, *tensor)
+    weights = [
+        P(dp, None, tensor),
+        P(tensor, dp),
+        P(dp, tensor),
+        P(dp, None, tensor),
+        P(tensor, dp),
+        P(dp, tensor),
+        P(tensor, dp),
+    ]
+    shared = [P(dp, None, None), P(None, dp), P(None, dp)]
+    taken = (P(both, None), *shared, *weights, P(both, None))
+    given = (P(both, None), P(both, None), *shared, *weights)
+    return taken, given
+
+
 def solution(mesh):
-    placed = (
-        P(("dp", "tensor"), None),
-        P("dp", None, None),
-        P(None, "dp"),
-        P(None, "dp"),
-        P("dp", None, "tensor"),
-        P("tensor", "dp"),
-        P("dp", "tensor"),
-        P("dp", None, "tensor"),
-        P("tensor", "dp"),
-        P("dp", "tensor"),
-        P("tensor", "dp"),
-        P(("dp", "tensor"), None),
-    )
-    return jax.shard_map(
-        on_device,
-        mesh=mesh,
-        in_specs=placed,
-        out_specs=(
-            P(("dp", "tensor"), None),
-            P(("dp", "tensor"), None),
-            P("dp", None, None),
-            P(None, "dp"),
-            P(None, "dp"),
-            P("dp", None, "tensor"),
-            P("tensor", "dp"),
-            P("dp", "tensor"),
-            P("dp", None, "tensor"),
-            P("tensor", "dp"),
-            P("dp", "tensor"),
-            P("tensor", "dp"),
-        ),
-        check_vma=False,
-    )
+    dp, tensor = mesh.shape["dp"], mesh.shape["tensor"]
+    if tensor == 2 and dp % 2 == 0:
+        body = on_pair
+        mesh = Mesh(mesh.devices.reshape(dp // 2, 2, 2), ("site", "core", "y"))
+        taken, given = placements(("site", "core"), ("y",))
+    else:
+        body = on_device
+        taken, given = placements(("dp",), ("tensor",))
+    return jax.shard_map(body, mesh=mesh, in_specs=taken, out_specs=given, check_vma=False)

time: 3410 us -> 1840 us (0.54)
  waiting for transfers between devices: 2270 us -> 1040 us
  matrix products: 671 us -> 323 us
  other arithmetic: 257 us -> 52 us
  starting transfers between devices: 2.14 us -> 160 us
  Pallas kernels: 0 us -> 139 us
  local copies, waits for them, and re-layouts: 119 us -> 36.8 us
    reduce_scatter x12 -> x6, waiting for transfers between devices: 1370 us -> 473 us  [share_grad(): lax.psum_scatter(low(grad), SPREAD, scatter_dimension=0, tiled=True)]
    all_gather x13 -> x7, waiting for transfers between devices: 682 us -> 255 us  [fetch(): return lax.all_gather(trade_corners(shard), SPREAD, axis=0, tiled=True)]
    dot_general x63 -> x27, matrix products: 671 us -> 323 us  [the longest x7 137 us: dot(): return jnp.dot(left, right, preferred_element_type=f32)]
    ppermute x0 -> x33, waiting for transfers between devices: none -> 214 us  [the longest x20 189 us: trade_corners(): return lax.ppermute(values, ('core', 'y'), [(0, 0), (1, 2), (2, 1), (3, 3)])]
    ppermute x0 -> x33, starting transfers between devices: none -> 149 us  [the longest x13 75.2 us: to_mate(): return lax.ppermute(values, 'core', [(0, 1), (1, 0)])]
    pallas_call x0 -> x4, Pallas kernels: none -> 139 us  [the longest x1 74.2 us: fused_self_back(): pl.pallas_call(functools.partial(self_back_kernel, min(ROWS_STEP, length)...]
    convert_element_type x21 -> x13, other arithmetic: 140 us -> 12.9 us  [the longest x10 11.1 us: low(): return values.astype(jnp.bfloat16)]
    unnamed x32 -> x15, waiting for transfers between devices: 192 us -> 97.6 us
  transfers between devices with their start and end apart: 29 -> 47, of which waited for: 28 -> 28; matrix products, arithmetic and copies ran while one was open for 13% -> 18% of each run, Pallas kernels for 0% -> 8%
where the time goes in v1:
time: 1840 us; the launch traced here: 1820 us
  waiting for transfers between devices  1040 us (57%)
  matrix products  323 us (18%)
  starting transfers between devices  160 us (9%)
  Pallas kernels  139 us (8%)
  blocking collectives  56.8 us (3%)
  other arithmetic  52 us (3%)
  local copies, waits for them, and re-layouts  36.8 us (2%)
    reduce_scatter x6, waiting for transfers between devices, share_grad(): lax.psum_scatter(low(grad), SPREAD, scatter_dimension=0, tiled=True)  473 us
    all_gather x7, waiting for transfers between devices, fetch(): return lax.all_gather(trade_corners(shard), SPREAD, axis=0, tiled=True)  255 us
    ppermute x20, waiting for transfers between devices, trade_corners(): return lax.ppermute(values, ('core', 'y'), [(0, 0), (1, 2), (2, 1), (3, 3)])  189 us
    dot_general x7, matrix products, dot(): return jnp.dot(left, right, preferred_element_type=f32)  137 us
    dot_general x13, matrix products, dot_last(): lax.dot_general(left, right, (((1,), (1,)), ((), ())), preferred_element_...  106 us
    unnamed x15, waiting for transfers between devices  97.6 us
    dot_general x7, matrix products, dot_first(): lax.dot_general(left, right, (((0,), (0,)), ((), ())), preferred_element_...  80.7 us
    ppermute x13, starting transfers between devices, to_mate(): return lax.ppermute(values, 'core', [(0, 1), (1, 0)])  75.2 us
  transfers between devices with their start and end apart: 47, of which 28 were waited for; matrix products, arithmetic and copies ran while one was open for 18% of the time, Pallas kernels for 8%

profile of v1, /device:TPU:1, one launch (start us, length us, event | category | flops | bytes accessed | tf_op | source)
XLA Modules:
  0.0 1822.5 jit_solution(6799562941157689323)
XLA Ops:
  8.6 4.5 collective-permute-start.2
  13.1 6.0 collective-permute-done.2
  33.1 6.2 collective-permute-done.8
  42.3 4.3 collective-permute-done.6
  52.9 82.4 %collective-permute-done.9 = bf16[96,768]{1,0:T(8,128)(2,1)S(1)} collective-permute-done((bf16[96,768]{1,0:T(8,128)(2,1)S(1)}, bf16[96,768]{1,0:T(8,128)(2,1)S(1)}, u32[]{:S(2)}, u32[]{:S(2)}) %collective-permute-start.9) | collective-permute-done | bytes 147488 | tf_op jit(solution)/shard_map/ppermute | solution.py:561
  136.1 17.7 all-gather
  163.4 6.7 collective-permute-start.12
  170.1 7.6 collective-permute-done.12
  178.6 5.3 broadcast_select_fusion.11
  183.9 17.8 convolution_convert_fusion.3.q_ref.k_ref.v_ref
  201.7 32.7 %attend_self.1 = (bf16[1536,768]{1,0:T(8,128)(2,1)}, f32[6,2,1536]{2,1,0:T(2,128)}) custom-call(bf16[1536,2304]{1,0:T(8,128)(2,1)} %convolution_convert_fusion.3.q_ref.k_ref.v_ref, bf16[1536,2304]{1,0:T(8,128)(2,1)} %convolution_convert_fusion.3.q_ref.k_ref.v_ref, bf16[1536,2304]{1,0:T(8,128)(2,1)} %convolution_convert_fusion.3.q_ref.k_ref.v_ref), custom_call_target="tpu_custom_call" | custom-call | flops 7247757312 | bytes 9437184 | tf_op jit(solution)/shard_map/attend_self/pallas_call | solution.py:476
  234.4 5.6 convolution_convert_fusion.13
  240.0 4.9 collective-permute-done.4
  244.9 5.6 fusion.73
  262.2 4.5 collective-permute-done.7
  266.7 19.5 %all-gather.15.cloned.1.call-done = bf16[1536,1536]{1,0:T(8,128)(2,1)} async-done(((bf16[96,1536]{1,0:T(8,128)(2,1)}), bf16[1536,1536]{1,0:T(8,128)(2,1)}) %all-gather.15.cloned.1.call-update) | async-done | bytes 4718608 | tf_op jit(solution)/shard_map/all_gather | solution.py:586
  290.3 4.3 broadcast_select_fusion.9
  294.7 55.5 %all-gather.13.cloned.1.call-done = bf16[1536,768]{1,0:T(8,128)(2,1)} async-done(((bf16[96,768]{1,0:T(8,128)(2,1)}), bf16[1536,768]{1,0:T(8,128)(2,1)}) %all-gather.13.cloned.1.call-update) | async-done | bytes 2359312 | tf_op jit(solution)/shard_map/all_gather | solution.py:586
  350.2 8.4 convolution_convert_fusion.12.q_ref
  358.6 12.9 attend_cross.1
  371.5 42.5 %all-gather.17.cloned.1.call-done = bf16[1536,768]{1,0:T(8,128)(2,1)} async-done(((bf16[96,768]{1,0:T(8,128)(2,1)}), bf16[1536,768]{1,0:T(8,128)(2,1)}) %all-gather.17.cloned.1.call-update) | async-done | bytes 2359312 | tf_op jit(solution)/shard_map/all_gather | solution.py:586
  414.0 5.5 convolution_convert_fusion.11
  424.3 12.8 collective-permute-done.13
  437.9 9.4 reduce-scatter.16.cloned.1.call-start
  447.5 7.1 fusion.74
  464.4 73.4 %all-gather.19.cloned.1.call-done = bf16[1536,3072]{1,0:T(8,128)(2,1)} async-done(((bf16[96,3072]{1,0:T(8,128)(2,1)}), bf16[1536,3072]{1,0:T(8,128)(2,1)}) %all-gather.19.cloned.1.call-update) | async-done | bytes 9437200 | tf_op jit(solution)/shard_map/all_gather | solution.py:586
  537.8 59.7 %multiply_convert_fusion = (bf16[1536,3072]{1,0:T(8,128)(2,1)}, f32[1536,3072]{1,0:T(8,128)}, f32[1536,3072]{1,0:T(8,128)}) fusion(bf16[1536,3072]{1,0:T(8,128)(2,1)} %all-gather.19.cloned.1.call-done, bf16[768,1536]{1,0:T(8,128)(2,1)} %get-tuple-element.104, bf16[768,1536]{1,0:T(8,128)(2,1)S(1)} %get-tuple-element.103), kind=kOutput, calls=%fused_computation.3 | convolution fusion | flops 14811660288 | bytes 61341696 | tf_op jit(solution)/shard_map/dot_general | solution.py:631
  597.5 63.6 %all-gather.21.cloned.1.call-done = bf16[1536,3072]{1,0:T(8,128)(2,1)} async-done(((bf16[96,3072]{1,0:T(8,128)(2,1)}), bf16[1536,3072]{1,0:T(8,128)(2,1)}) %all-gather.21.cloned.1.call-update) | async-done | bytes 9437200 | tf_op jit(solution)/shard_map/all_gather | solution.py:586
  661.1 29.9 %add_convert_fusion = bf16[1536,3072]{1,0:T(8,128)(2,1)} fusion(f32[1536,3072]{1,0:T(8,128)} %get-tuple-element.96, f32[1536,3072]{1,0:T(8,128)} %get-tuple-element.115, bf16[1536,3072]{1,0:T(8,128)(2,1)} %all-gather.21.cloned.1.call-done, bf16[768,1536]{1,0:T(8,128)(2,1)} %get-tuple-element.102, bf16[768,1536]{1,0:T(8,128)(2,1)} %get-tuple-element.101), kind=kOutput, calls=%fused_computation.2 | convolution fusion | flops 14571012096 | bytes 61341696 | tf_op jit(solution)/shard_map/dot_general | solution.py:631
  691.1 11.7 fusion.28
  709.0 13.2 multiply_reduce_fusion
  733.4 5.2 convolution_convert_fusion.5
  738.7 8.3 convolution_convert_fusion.10.grad_ref
  747.0 19.4 %attend_cross_back.1 = (bf16[1536,768]{1,0:T(8,128)(2,1)}, bf16[64,768]{1,0:T(8,128)(2,1)}, bf16[64,768]{1,0:T(8,128)(2,1)}) custom-call(bf16[1536,768]{1,0:T(8,128)(2,1)} %convolution_convert_fusion.12.q_ref, bf16[64,1536]{1,0:T(8,128)(2,1)} %convolution_convert_fusion.14.k_ref.v_ref, bf16[64,1536]{1,0:T(8,128)(2,1)} %convolution_convert_fusion.14.k_ref.v_ref, ...), custom_call_target="tpu_custom_call" | custom-call | flops 754974720 | bytes 12288000 | tf_op jit(solution)/shard_map/attend_cross_back/pallas_call | solution.py:530
  766.4 8.4 convolution_convert_fusion.6
  774.8 20.8 %convolution_convert_fusion = bf16[1536,3072]{1,0:T(8,128)(2,1)} fusion(bf16[1536,3072]{1,0:T(8,128)(2,1)} %get-tuple-element.95, bf16[768,1536]{1,0:T(8,128)(2,1)} %get-tuple-element.102, bf16[768,1536]{1,0:T(8,128)(2,1)} %get-tuple-element.101), kind=kOutput, calls=%fused_computation.17 | convolution fusion | flops 14509670400 | bytes 23592960 | tf_op jit(solution)/shard_map/dot_general | solution.py:311
  795.8 20.4 %convolution_convert_fusion.1 = bf16[1536,3072]{1,0:T(8,128)(2,1)} fusion(bf16[1536,3072]{1,0:T(8,128)(2,1)} %add_convert_fusion, bf16[768,1536]{1,0:T(8,128)(2,1)} %get-tuple-element.104, bf16[768,1536]{1,0:T(8,128)(2,1)} %copy-done.9), kind=kOutput, calls=%fused_computation.18 | convolution fusion | flops 14509670400 | bytes 23592960 | tf_op jit(solution)/shard_map/dot_general | solution.py:311
  820.7 6.6 copy.38
  836.8 5.0 multiply_reduce_fusion.1
  852.9 5.2 convolution_convert_fusion.7
  858.2 8.4 convolution_convert_fusion.8.grad_ref
  866.6 74.2 %attend_self_back.1 = bf16[1536,2304]{1,0:T(8,128)(2,1)} custom-call(bf16[1536,2304]{1,0:T(8,128)(2,1)} %convolution_convert_fusion.3.q_ref.k_ref.v_ref, bf16[1536,2304]{1,0:T(8,128)(2,1)} %convolution_convert_fusion.3.q_ref.k_ref.v_ref, bf16[1536,2304]{1,0:T(8,128)(2,1)} %convolution_convert_fusion.3.q_ref.k_ref.v_ref, ...), custom_call_target="tpu_custom_call" | custom-call | flops 18119393280 | bytes 23592960 | tf_op jit(solution)/shard_map/attend_self_back/pallas_call | solution.py:507
  940.8 17.1 convolution_convert_fusion.2
  957.9 11.9 fusion.25
  970.2 10.3 fusion.22
  980.7 13.3 add_add_fusion.6
  997.6 10.7 multiply_reduce_fusion.2
  1012.0 4.7 add_add_fusion.3
  1021.0 68.8 %collective-permute-start.24 = (f32[64,1536]{1,0:T(8,128)S(1)}, f32[64,1536]{1,0:T(8,128)S(1)}, u32[]{:S(2)}, u32[]{:S(2)}) collective-permute-start(f32[64,1536]{1,0:T(8,128)S(1)} %fusion.75), channel_id=1, source_target_pairs={{0,2},{2,0},{1,3},{3,1},{4,6},{6,4},{5,7},{7,5},{8,10},{10,8},{9,1... | collective-permute-start | bytes 1179656 | tf_op jit(solution)/shard_map/ppermute | solution.py:565
  1096.9 55.2 %collective-permute-done.25 = f32[64,1536]{1,0:T(8,128)S(1)} collective-permute-done((f32[64,1536]{1,0:T(8,128)S(1)}, f32[64,1536]{1,0:T(8,128)S(1)}, u32[]{:S(2)}, u32[]{:S(2)}) %collective-permute-start.25) | collective-permute-done | bytes 393248 | tf_op jit(solution)/shard_map/ppermute | solution.py:561
  1154.5 29.4 %reduce-scatter.20.cloned.1.call-done = bf16[96,3072]{1,0:T(8,128)(2,1)} async-done(((bf16[1536,3072]{1,0:T(8,128)(2,1)}), bf16[96,3072]{1,0:T(8,128)(2,1)}) %reduce-scatter.20.cloned.1.call-update) | async-done | bytes 589840 | tf_op jit(solution)/shard_map/reduce_scatter | solution.py:590
  1183.9 4.4 collective-permute-start.32
  1188.3 172.1 %reduce-scatter.18.cloned.1.call-done = bf16[96,3072]{1,0:T(8,128)(2,1)} async-done(((bf16[1536,3072]{1,0:T(8,128)(2,1)}), bf16[96,3072]{1,0:T(8,128)(2,1)}) %reduce-scatter.18.cloned.1.call-update) | async-done | bytes 589840 | tf_op jit(solution)/shard_map/reduce_scatter | solution.py:590
  1360.4 4.4 collective-permute-start.31
  1366.4 39.1 %psum.7 = f32[6,1536]{1,0:T(8,128)S(1)} all-reduce(f32[6,1536]{1,0:T(8,128)S(1)} %stack.2), channel_id=1, replica_groups=mesh['site'=8,'core'=2,'y'=2] {'site','core','y'}, use_global_device_ids=true, to_apply=%region_18.19 | all-reduce | flops 9216 | bytes 73728 | tf_op jit(solution)/shard_map/psum | solution.py:680
  1405.6 97.4 %reduce-scatter.22.cloned.1.call-done = bf16[96,1536]{1,0:T(8,128)(2,1)} async-done(((bf16[1536,1536]{1,0:T(8,128)(2,1)}), bf16[96,1536]{1,0:T(8,128)(2,1)}) %reduce-scatter.22.cloned.1.call-update) | async-done | bytes 294928
  1504.2 5.4 collective-permute-start.29
  1509.6 126.2 %reduce-scatter.12.cloned.1.call-done = bf16[96,768]{1,0:T(8,128)(2,1)} async-done(((bf16[1536,768]{1,0:T(8,128)(2,1)}), bf16[96,768]{1,0:T(8,128)(2,1)}) %reduce-scatter.12.cloned.1.call-update) | async-done | bytes 147472 | tf_op jit(solution)/shard_map/reduce_scatter | solution.py:590
  1635.7 5.5 collective-permute-start.27
  1647.1 145.3 %reduce-scatter.10.cloned.1.call-done = bf16[96,2304]{1,0:T(8,128)(2,1)} async-done(((bf16[1536,2304]{1,0:T(8,128)(2,1)}), bf16[96,2304]{1,0:T(8,128)(2,1)}) %reduce-scatter.10.cloned.1.call-update) | async-done | bytes 442384 | tf_op jit(solution)/shard_map/reduce_scatter | solution.py:590
  1792.4 5.4 collective-permute-start.26
  1799.0 5.1 collective-permute-done.26
  1805.1 4.8 copy.50
  1809.9 4.8 copy.51
  (306 shorter events, 142.2 us)
Async XLA Ops:
  7.2 32.9 %copy-start.22 = (f32[96,768]{1,0:T(8,128)S(1)}, f32[96,768]{1,0:T(8,128)}, u32[]{:S(2)}) copy-start(f32[96,768]{1,0:T(8,128)} %param.18) | copy-start | bytes 884740
  7.2 42.3 %copy-start.23 = (f32[768,96]{0,1:T(8,128)S(1)}, f32[768,96]{0,1:T(8,128)}, u32[]{:S(2)}) copy-start(f32[768,96]{0,1:T(8,128)} %param.20) | copy-start | bytes 884740
  7.2 128.9 %copy-start.56 = (f32[3,96]{1,0:T(4,128)S(1)}, f32[3,96]{1,0:T(4,128)}, u32[]{:S(2)}) copy-start(f32[3,96]{1,0:T(4,128)} %param.14) | copy-start | bytes 3460
  7.2 128.9 %copy-start.57 = (f32[3,96]{1,0:T(4,128)S(1)}, f32[3,96]{1,0:T(4,128)}, u32[]{:S(2)}) copy-start(f32[3,96]{1,0:T(4,128)} %param.15) | copy-start | bytes 3460
  7.2 176.6 %all-gather.9.cloned.1.call-start = ((), (), s32[]{:S(2)}) async-start(), calls=%async_computation.7 | async-start | bytes 7520256 | tf_op jit(solution)/shard_map/all_gather | solution.py:586
  8.6 10.5 collective-permute-start.2
  19.9 214.5 %all-gather.11.cloned.1.call-start = ((), (), s32[]{:S(2)}) async-start(), calls=%async_computation.8 | async-start | bytes 2506752 | tf_op jit(solution)/shard_map/all_gather | solution.py:586
  20.9 6.5 collective-permute-start.3
  28.0 258.1 %all-gather.15.cloned.1.call-start = ((), (), s32[]{:S(2)}) async-start(), calls=%async_computation.10 | async-start | bytes 5013504 | tf_op jit(solution)/shard_map/all_gather | solution.py:586
  29.4 9.9 collective-permute-start.8
  40.0 310.1 %all-gather.13.cloned.1.call-start = ((), (), s32[]{:S(2)}) async-start(), calls=%async_computation.9 | async-start | bytes 2506752 | tf_op jit(solution)/shard_map/all_gather | solution.py:586
  40.1 6.5 collective-permute-start.6
  47.3 366.7 %all-gather.17.cloned.1.call-start = ((), (), s32[]{:S(2)}) async-start(), calls=%async_computation.11 | async-start | bytes 2506752 | tf_op jit(solution)/shard_map/all_gather | solution.py:586
  47.3 106.7 %collective-permute-start = (f32[768,1536]{1,0:T(8,128)}, f32[768,1536]{1,0:T(8,128)}, u32[]{:S(2)}, u32[]{:S(2)}) collective-permute-start(f32[768,1536]{1,0:T(8,128)} %param.12), channel_id=1, source_target_pairs={{0,0},{1,2},{2,1},{3,3},{4,4},{5,6},{6,5},{7,7},{8,8},{9,10},{10,9... | collective-permute-start | bytes 14155784 | tf_op jit(solution)/shard_map/ppermute | solution.py:561
  49.5 85.8 %collective-permute-start.9 = (bf16[96,768]{1,0:T(8,128)(2,1)S(1)}, bf16[96,768]{1,0:T(8,128)(2,1)S(1)}, u32[]{:S(2)}, u32[]{:S(2)}) collective-permute-start(bf16[96,768]{1,0:T(8,128)(2,1)S(1)} %convert_bitcast_fusion.6), channel_id=1, source_target_pairs={{0,0},{1,2},{2,1},{3,3},{4,4},{5,6},{6,5},{7,7},{8,8},{9,10},{10,9... | collective-permute-start | bytes 442376 | tf_op jit(solution)/shard_map/ppermute | solution.py:561
  136.0 401.8 %all-gather.19.cloned.1.call-start = ((), (), s32[]{:S(2)}) async-start(), calls=%async_computation.12 | async-start | bytes 10027008 | tf_op jit(solution)/shard_map/all_gather | solution.py:586
  154.0 24.6 %copy-start.28 = (f32[1536]{0:T(1024)}, f32[1536]{0:T(1024)S(1)}, u32[]{:S(2)}) copy-start(f32[1536]{0:T(1024)S(1)} %get-tuple-element.88) | copy-start | bytes 18436
  154.0 136.3 %copy-start.30 = (f32[1536]{0:T(1024)}, f32[1536]{0:T(1024)S(1)}, u32[]{:S(2)}) copy-start(f32[1536]{0:T(1024)S(1)} %get-tuple-element.86) | copy-start | bytes 18436
  154.0 307.7 %copy-start.32 = (f32[1536]{0:T(1024)}, f32[1536]{0:T(1024)S(1)}, u32[]{:S(2)}) copy-start(f32[1536]{0:T(1024)S(1)} %get-tuple-element.83) | copy-start | bytes 18436
  162.9 15.7 collective-permute-start.1
  163.4 14.3 collective-permute-start.12
  178.5 482.6 %all-gather.21.cloned.1.call-start = ((), (), s32[]{:S(2)}) async-start(), calls=%async_computation.13 | async-start | bytes 10027008 | tf_op jit(solution)/shard_map/all_gather | solution.py:586
  240.0 4.9 collective-permute-start.4
  250.5 39.8 %copy-start.36 = (f32[768]{0:T(1024)}, f32[768]{0:T(1024)S(1)}, u32[]{:S(2)}) copy-start(f32[768]{0:T(1024)S(1)} %broadcast_multiply_fusion.1) | copy-start | bytes 9220
  251.2 39.1 %copy-start.44 = (f32[768]{0:T(1024)}, f32[768]{0:T(1024)S(1)}, u32[]{:S(2)}) copy-start(f32[768]{0:T(1024)S(1)} %fusion.41) | copy-start | bytes 9220
  254.0 36.3 %collective-permute-start.5 = (bf16[768,1536]{1,0:T(8,128)(2,1)}, bf16[768,1536]{1,0:T(8,128)(2,1)}, u32[]{:S(2)}, u32[]{:S(2)}) collective-permute-start(bf16[768,1536]{1,0:T(8,128)(2,1)} %add_convert_fusion.2), channel_id=1, source_target_pairs={{0,2},{2,0},{1,3},{3,1},{4,6},{6,4},{5,7},{7,5},{8,10},{10,8},{9,1... | collective-permute-start | bytes 7077896 | tf_op jit(solution)/shard_map/ppermute | solution.py:565
  255.0 11.7 collective-permute-start.7
  260.3 187.1 %collective-permute-start.16 = (bf16[768,1536]{1,0:T(8,128)(2,1)}, bf16[768,1536]{1,0:T(8,128)(2,1)S(1)}, u32[]{:S(2)}, u32[]{:S(2)}) collective-permute-start(bf16[768,1536]{1,0:T(8,128)(2,1)} %convert_element_type.167), channel_id=1, source_target_pairs={{0,0},{1,2},{2,1},{3,3},{4,4},{5,6},{6,5},{7,7},{8,8},{9,10},{10,9... | collective-permute-start | bytes 7077896 | tf_op jit(solution)/shard_map/ppermute | solution.py:561
  266.7 28.0 %copy-start.16 = (bf16[64,1536]{1,0:T(8,128)(2,1)}, bf16[64,1536]{1,0:T(8,128)(2,1)S(1)}, u32[]{:S(2)}) copy-start(bf16[64,1536]{1,0:T(8,128)(2,1)S(1)} %collective-permute-done.7) | copy-start | bytes 589828
  419.5 28.0 %collective-permute-start.10 = (bf16[768,1536]{1,0:T(8,128)(2,1)}, bf16[768,1536]{1,0:T(8,128)(2,1)}, u32[]{:S(2)}, u32[]{:S(2)}) collective-permute-start(bf16[768,1536]{1,0:T(8,128)(2,1)} %convolution_convert_fusion.11), channel_id=1, source_target_pairs={{0,2},{2,0},{1,3},{3,1},{4,6},{6,4},{5,7},{7,5},{8,10},{10,8},{9,1... | collective-permute-start | bytes 7077896 | tf_op jit(solution)/shard_map/ppermute | solution.py:565
  421.3 15.8 collective-permute-start.13
  437.9 656.4 %reduce-scatter.16.cloned.1.call-start = ((), (), s32[]{:S(2)}) async-start(), calls=%async_computation.17 | async-start | bytes 2506752 | tf_op jit(solution)/shard_map/reduce_scatter | solution.py:590
  447.4 9.8 collective-permute-start.17
  457.1 4.6 collective-permute-start.11
  464.4 133.1 %copy-start.9 = (bf16[768,1536]{1,0:T(8,128)(2,1)}, bf16[768,1536]{1,0:T(8,128)(2,1)S(1)}, u32[]{:S(2)}) copy-start(bf16[768,1536]{1,0:T(8,128)(2,1)S(1)} %get-tuple-element.103) | copy-start | bytes 7077892
  702.7 6.2 collective-permute-start.18
  726.3 4.5 collective-permute-start.19
  738.6 413.5 %reduce-scatter.14.cloned.1.call-start = ((), (), s32[]{:S(2)}) async-start(), calls=%async_computation.16 | async-start | bytes 2506752 | tf_op jit(solution)/shard_map/reduce_scatter | solution.py:590
  774.8 409.1 %reduce-scatter.20.cloned.1.call-start = ((), (), s32[]{:S(2)}) async-start(), calls=%async_computation.19 | async-start | bytes 10027008 | tf_op jit(solution)/shard_map/reduce_scatter | solution.py:590
  795.7 564.7 %reduce-scatter.18.cloned.1.call-start = ((), (), s32[]{:S(2)}) async-start(), calls=%async_computation.18 | async-start | bytes 10027008 | tf_op jit(solution)/shard_map/reduce_scatter | solution.py:590
  816.2 686.8 %reduce-scatter.22.cloned.1.call-start = ((), (), s32[]{:S(2)}) async-start(), calls=%async_computation.20 | async-start | bytes 5013504
  827.4 808.3 %reduce-scatter.12.cloned.1.call-start = ((), (), s32[]{:S(2)}) async-start(), calls=%async_computation.15 | async-start | bytes 2506752 | tf_op jit(solution)/shard_map/reduce_scatter | solution.py:590
  832.2 4.7 collective-permute-start.20
  845.8 4.6 collective-permute-start.21
  858.1 934.3 %reduce-scatter.10.cloned.1.call-start = ((), (), s32[]{:S(2)}) async-start(), calls=%async_computation.14 | async-start | bytes 7520256 | tf_op jit(solution)/shard_map/reduce_scatter | solution.py:590
  957.9 22.8 %slice-start.6 = ((s8[4718592]{0:T(1024)(128)(4,1)}), s8[524288]{0:T(1024)(128)(4,1)S(1)}, s32[]{:S(2)}) async-start(s8[4718592]{0:T(1024)(128)(4,1)} %bitcast.73), calls=%async_computation.27 | async-start | bytes 1048576
  957.9 22.8 %slice-start.7 = ((s8[4718592]{0:T(1024)(128)(4,1)}), s8[4194304]{0:T(1024)(128)(4,1)S(1)}, s32[]{:S(2)}) async-start(s8[4718592]{0:T(1024)(128)(4,1)} %bitcast.73), calls=%async_computation.28 | async-start | bytes 8388608
  969.8 10.9 collective-permute-start.14
  970.2 41.8 %slice-start.2 = ((s8[4718592]{0:T(1024)(128)(4,1)}), s8[4194304]{0:T(1024)(128)(4,1)S(1)}, s32[]{:S(2)}) async-start(s8[4718592]{0:T(1024)(128)(4,1)} %bitcast.69), calls=%async_computation.23 | async-start | bytes 8388608
  980.5 31.5 %slice-start.3 = ((s8[4718592]{0:T(1024)(128)(4,1)}), s8[524288]{0:T(1024)(128)(4,1)S(1)}, s32[]{:S(2)}) async-start(s8[4718592]{0:T(1024)(128)(4,1)} %bitcast.69), calls=%async_computation.24 | async-start | bytes 1048576
  980.5 17.1 collective-permute-start.22
  994.1 158.0 %collective-permute-start.15 = (f32[768,1536]{1,0:T(8,128)}, f32[768,1536]{1,0:T(8,128)}, u32[]{:S(2)}, u32[]{:S(2)}) collective-permute-start(f32[768,1536]{1,0:T(8,128)} %add_add_fusion.6), channel_id=1, source_target_pairs={{0,0},{1,2},{2,1},{3,3},{4,4},{5,6},{6,5},{7,7},{8,8},{9,10},{10,9... | collective-permute-start | bytes 14155784 | tf_op jit(solution)/shard_map/ppermute | solution.py:561
  1016.7 80.1 %copy-start.55 = (f32[1536]{0:T(1024)S(1)}, f32[1536]{0:T(1024)}, u32[]{:S(2)}) copy-start(f32[1536]{0:T(1024)} %get-tuple-element.74) | copy-start | bytes 18436
  1016.7 80.2 %copy-start.54 = (f32[1536]{0:T(1024)S(1)}, f32[1536]{0:T(1024)}, u32[]{:S(2)}) copy-start(f32[1536]{0:T(1024)} %get-tuple-element.80) | copy-start | bytes 18436
  1016.7 629.3 %collective-permute-start.23 = (f32[768,1536]{1,0:T(8,128)}, f32[768,1536]{1,0:T(8,128)}, u32[]{:S(2)}, u32[]{:S(2)}) collective-permute-start(f32[768,1536]{1,0:T(8,128)} %add_add_fusion.3), channel_id=1, source_target_pairs={{0,0},{1,2},{2,1},{3,3},{4,4},{5,6},{6,5},{7,7},{8,8},{9,10},{10,9... | collective-permute-start | bytes 14155784 | tf_op jit(solution)/shard_map/ppermute | solution.py:561
  1021.0 70.2 %collective-permute-start.24 = (f32[64,1536]{1,0:T(8,128)S(1)}, f32[64,1536]{1,0:T(8,128)S(1)}, u32[]{:S(2)}, u32[]{:S(2)}) collective-permute-start(f32[64,1536]{1,0:T(8,128)S(1)} %fusion.75), channel_id=1, source_target_pairs={{0,2},{2,0},{1,3},{3,1},{4,6},{6,4},{5,7},{7,5},{8,10},{10,8},{9,1... | collective-permute-start | bytes 1179656 | tf_op jit(solution)/shard_map/ppermute | solution.py:565
  1091.2 60.8 %collective-permute-start.25 = (f32[64,1536]{1,0:T(8,128)S(1)}, f32[64,1536]{1,0:T(8,128)S(1)}, u32[]{:S(2)}, u32[]{:S(2)}) collective-permute-start(f32[64,1536]{1,0:T(8,128)S(1)} %add.166), channel_id=1, source_target_pairs={{0,0},{1,2},{2,1},{3,3},{4,4},{5,6},{6,5},{7,7},{8,8},{9,10},{10,9... | collective-permute-start | bytes 1179656 | tf_op jit(solution)/shard_map/ppermute | solution.py:561
  1094.4 270.5 %collective-permute-start.30 = (bf16[96,768]{1,0:T(8,128)(2,1)}, bf16[96,768]{1,0:T(8,128)(2,1)S(1)}, u32[]{:S(2)}, u32[]{:S(2)}) collective-permute-start(bf16[96,768]{1,0:T(8,128)(2,1)} %reduce-scatter.16.cloned.1.call-done), channel_id=1, source_target_pairs={{0,0},{1,2},{2,1},{3,3},{4,4},{5,6},{6,5},{7,7},{8,8},{9,10},{10,9... | collective-permute-start | bytes 442376 | tf_op jit(solution)/shard_map/ppermute | solution.py:561
  1152.1 213.5 %collective-permute-start.28 = (bf16[96,768]{1,0:T(8,128)(2,1)}, bf16[96,768]{1,0:T(8,128)(2,1)S(1)}, u32[]{:S(2)}, u32[]{:S(2)}) collective-permute-start(bf16[96,768]{1,0:T(8,128)(2,1)} %reduce-scatter.14.cloned.1.call-done), channel_id=1, source_target_pairs={{0,0},{1,2},{2,1},{3,3},{4,4},{5,6},{6,5},{7,7},{8,8},{9,10},{10,9... | collective-permute-start | bytes 442376 | tf_op jit(solution)/shard_map/ppermute | solution.py:561
  1183.9 614.0 %collective-permute-start.32 = (bf16[96,3072]{1,0:T(8,128)(2,1)}, bf16[96,3072]{1,0:T(8,128)(2,1)S(1)}, u32[]{:S(2)}, u32[]{:S(2)}) collective-permute-start(bf16[96,3072]{1,0:T(8,128)(2,1)} %reduce-scatter.20.cloned.1.call-done), channel_id=1, source_target_pairs={{0,0},{1,2},{2,1},{3,3},{4,4},{5,6},{6,5},{7,7},{8,8},{9,10},{10,9... | collective-permute-start | bytes 1769480 | tf_op jit(solution)/shard_map/ppermute | solution.py:561
  1360.4 285.6 %collective-permute-start.31 = (bf16[96,3072]{1,0:T(8,128)(2,1)}, bf16[96,3072]{1,0:T(8,128)(2,1)S(1)}, u32[]{:S(2)}, u32[]{:S(2)}) collective-permute-start(bf16[96,3072]{1,0:T(8,128)(2,1)} %reduce-scatter.18.cloned.1.call-done), channel_id=1, source_target_pairs={{0,0},{1,2},{2,1},{3,3},{4,4},{5,6},{6,5},{7,7},{8,8},{9,10},{10,9... | collective-permute-start | bytes 1769480 | tf_op jit(solution)/shard_map/ppermute | solution.py:561
  1504.2 140.8 %collective-permute-start.29 = (bf16[96,1536]{0,1:T(8,128)(2,1)S(1)}, bf16[96,1536]{0,1:T(8,128)(2,1)S(1)}, u32[]{:S(2)}, u32[]{:S(2)}) collective-permute-start(bf16[96,1536]{0,1:T(8,128)(2,1)S(1)} %copy.39), channel_id=1, source_target_pairs={{0,0},{1,2},{2,1},{3,3},{4,4},{5,6},{6,5},{7,7},{8,8},{9,10},{10,9... | collective-permute-start | bytes 884744 | tf_op jit(solution)/shard_map/ppermute | solution.py:561
  1635.7 8.6 collective-permute-start.27
  1792.4 11.6 collective-permute-start.26
  (58 other events, 484.8 us)
Sparse Core Ops, SparseCore 0:
  20.0 113.2 all-gather.8
  136.7 60.9 all-gather.10
  201.0 85.1 all-gather.14
  289.4 60.7 all-gather.12
  353.4 60.5 all-gather.16
  417.2 120.5 all-gather.18
  541.2 119.9 all-gather.20
  738.7 124.9 reduce-scatter.15
  868.6 127.9 reduce-scatter.13
  1002.2 181.6 reduce-scatter.19
  1189.6 170.7 reduce-scatter.17
  1365.4 137.5 reduce-scatter.21
  1507.9 127.7 reduce-scatter.11
  1640.9 151.4 reduce-scatter.9

commit v2 on v1

--- a/solution.py
+++ b/solution.py
@@ -550,19 +550,21 @@
     )(queries, text_pair, text_pair, grads, logs)
 
 
-SPREAD = ("site", "y")
-
-
 def low(values):
     return values.astype(jnp.bfloat16)
 
 
+def at_corner():
+    return lax.axis_index("core") != lax.axis_index("y")
+
+
 def trade_corners(values):
-    return lax.ppermute(values, ("core", "y"), [(0, 0), (1, 2), (2, 1), (3, 3)])
-
-
-def to_mate(values):
-    return lax.ppermute(values, "core", [(0, 1), (1, 0)])
+    received = lax.ppermute(values, ("core", "y"), [(1, 2), (2, 1)])
+    return jnp.where(at_corner(), received, values)
+
+
+def to_mate(values, axis="core"):
+    return lax.ppermute(values, axis, [(0, 1), (1, 0)])
 
 
 def gather_pair(local_rows):
@@ -582,13 +584,74 @@
     return mine + received.astype(jnp.float32)
 
 
+ORDERS = (("x", "y"), ("y", "x"))
+
+
 def fetch(shard):
-    return lax.all_gather(trade_corners(shard), SPREAD, axis=0, tiled=True)
-
-
-def share_grad(grad):
-    summed = lax.psum_scatter(low(grad), SPREAD, scatter_dimension=0, tiled=True)
-    return trade_corners(summed).astype(jnp.float32)
+    line = lax.all_gather(shard, "z", axis=0)
+    count, rows, columns = line.shape
+    width = columns // 2
+    whole = jnp.broadcast_to(line[:, None, None], (count, 2, 2, rows, columns))
+    for start, order in zip((0, width), ORDERS):
+        here = {axis: lax.axis_index(axis) for axis in order}
+        pieces = [(line[:, :, start : start + width].reshape(-1, width), here)]
+        for axis in order:
+            pieces += [
+                (to_mate(piece, axis), {**place, axis: 1 - place[axis]}) for piece, place in pieces
+            ]
+        for piece, place in pieces[1:]:
+            whole = lax.dynamic_update_slice(
+                whole,
+                piece.reshape(count, 1, 1, rows, width),
+                (0, place["x"], place["y"], 0, start),
+            )
+    return whole.reshape(-1, columns)
+
+
+def halve(grad, order):
+    depth, columns = grad.shape
+    block = grad.reshape(lax.axis_size("z"), 2, 2, -1, columns)
+    dims = (1, 1) if order[0] == "x" else (2, 1)
+    for axis, dim in zip(order, dims):
+        here = lax.axis_index(axis)
+        theirs = lax.dynamic_index_in_dim(block, 1 - here, dim, keepdims=False)
+        kept = lax.dynamic_index_in_dim(block, here, dim, keepdims=False)
+        received = to_mate(theirs.reshape(-1, columns), axis).reshape(kept.shape)
+        block = low(kept.astype(jnp.float32) + received.astype(jnp.float32))
+    return block
+
+
+def start_sums(left, right):
+    width = right.shape[1] // 2
+    return [
+        halve(low(dot_first(left, right[:, start : start + width])), order)
+        for start, order in zip((0, width), ORDERS)
+    ]
+
+
+def share_grads(started):
+    joined = jnp.concatenate([part for parts in started for part in parts], axis=2)
+    summed = lax.psum_scatter(joined, "z", scatter_dimension=0, tiled=True)[0]
+    summed = trade_corners(summed).astype(jnp.float32)
+    ends = [0]
+    for parts in started:
+        ends.append(ends[-1] + sum(part.shape[2] for part in parts))
+    return [summed[:, start:end] for start, end in zip(ends, ends[1:])]
+
+
+def after(values, *others):
+    return lax.optimization_barrier((values, *others))[0]
+
+
+def sum_everywhere(values):
+    for axis in ("core", "x", "y"):
+        values = values + to_mate(values, axis)
+    count = lax.axis_size("z")
+    step = 1
+    while step < count:
+        values = values + lax.ppermute(values, "z", [(i, i ^ step) for i in range(count)])
+        step *= 2
+    return values
 
 
 def on_pair(
@@ -608,20 +671,35 @@
     depth, _, lanes = self_qkv.shape
     pairs = lanes // PAIR
     f32 = jnp.float32
-    norms = lax.all_gather(
-        low(jnp.concatenate([norm_gains, norm_biases], axis=0)), ("site", "core"), axis=1, tiled=True
-    ).astype(f32)
+    norm_shard = low(jnp.concatenate([norm_gains, norm_biases], axis=0)).T
+    norm_shard = jnp.pad(norm_shard, ((0, 0), (0, 2 * PAIR - norm_shard.shape[1])))
+    pieces = [
+        low(self_qkv).reshape(depth, 3 * lanes),
+        norm_shard,
+        low(self_out).T,
+        low(cross_query),
+        low(cross_kv).reshape(depth, 2 * lanes),
+        low(cross_out).T,
+        low(mlp_up),
+        low(mlp_down).T,
+    ]
+    shard_one = trade_corners(jnp.concatenate(pieces[:2], axis=1))
+    shard = trade_corners(jnp.concatenate(pieces[2:], axis=1))
+    second = 5 * lanes
+    third = second + mlp_up.shape[1]
+    pack_one = fetch(shard_one)
+    rows = trade_corners(after(states, shard))
+    text_low = trade_corners(after(low(text_states[0]), shard))
+    pack_two = fetch(shard[:, :second])
+    w_up = fetch(shard[:, second:third])
+    w_down = fetch(shard[:, third:])
+    w_qkv = pack_one[:, : 3 * lanes]
+    norms = pack_one[:, 3 * lanes : 3 * lanes + 6].T.astype(f32)
     gains, biases = norms[:3], norms[3:]
-    w_qkv = fetch(low(self_qkv).reshape(depth, 3 * lanes))
-    w_self_out = fetch(low(self_out).T)
-    w_kv = fetch(low(cross_kv).reshape(depth, 2 * lanes))
-    w_query = fetch(low(cross_query))
-    w_cross_out = fetch(low(cross_out).T)
-    w_up = fetch(low(mlp_up))
-    w_down = fetch(low(mlp_down).T)
-    rows = trade_corners(states)
-    text_low = trade_corners(low(text_states[0]))
-    grad_rows = trade_corners(low(out_grad))
+    w_self_out = pack_two[:, :lanes]
+    w_query = pack_two[:, lanes : 2 * lanes]
+    w_kv = pack_two[:, 2 * lanes : 4 * lanes]
+    w_cross_out = pack_two[:, 4 * lanes :]
 
     def norm_back(values, which, grads):
         _, pull = jax.vjp(normalize, values, gains[which], biases[which])
@@ -633,6 +711,7 @@
     normed_one = gather_pair(low(normalize(rows, gains[0], biases[0])))
     triple = low(dot(normed_one, w_qkv))
     self_mixed, self_logs = fused_attend(triple, triple, pairs, 2 * pairs, lanes, True)
+    grad_rows = trade_corners(after(low(out_grad), self_logs))
     after_self = rows + scatter_pair(self_mixed, lambda part: dot_last(part, w_self_out))
     normed_two = gather_pair(low(normalize(after_self, gains[1], biases[1])))
     queries = low(dot(normed_two, w_query))
@@ -641,45 +720,56 @@
     after_cross = after_self + scatter_pair(cross_mixed, lambda part: dot_last(part, w_cross_out))
     normed_three = gather_pair(low(normalize(after_cross, gains[2], biases[2])))
     hidden_pre = dot(normed_three, w_up)
-    hidden = low(activate(hidden_pre))
-    layer_out = trade_corners(
-        after_cross + scatter_pair(hidden, lambda part: dot_last(part, w_down))
+    chance = 0.5 + 0.5 * lax.erf(hidden_pre * math.sqrt(0.5))
+    hidden = low(hidden_pre * chance)
+    slope = low(
+        chance + hidden_pre * jnp.exp(-0.5 * hidden_pre * hidden_pre) / math.sqrt(2 * math.pi)
     )
     branch_grads = gather_pair(grad_rows)
-    down_grad = share_grad(dot_first(branch_grads, hidden)).T
-    hidden_grad = dot(branch_grads, w_down)
-    _, pull_act = jax.vjp(activate, hidden_pre)
-    pre_grad = low(pull_act(hidden_grad)[0])
-    up_grad = share_grad(dot_first(normed_three, pre_grad))
+    (down_grad,) = share_grads([start_sums(branch_grads, hidden)])
+    layer_out = low(after_cross + scatter_pair(hidden, lambda part: dot_last(part, w_down)))
+    pre_grad = low(dot(branch_grads, w_down) * slope.astype(f32))
+    (up_grad,) = share_grads([start_sums(normed_three, pre_grad)])
     back_three = scatter_pair(pre_grad, lambda part: dot_last(part, w_up))
     rows_three, gain_three, shift_three = norm_back(after_cross, 2, back_three)
     cross_rows_grad = grad_rows.astype(f32) + rows_three
     cross_grads = gather_pair(low(cross_rows_grad))
-    cross_out_grad = share_grad(dot_first(cross_grads, cross_mixed)).T
     cross_mixed_grad = low(dot(cross_grads, w_cross_out))
     query_grad, key_grad, value_grad = fused_cross_back(
         queries, text_pair, cross_logs, cross_mixed_grad
     )
     pair_grad = jnp.concatenate([key_grad, value_grad], axis=1)
-    query_weight_grad = share_grad(dot_first(normed_two, query_grad))
-    kv_weight_grad = share_grad(dot_first(text_low, pair_grad)).reshape(depth, 2, lanes)
     text_part = dot_last(pair_grad, w_kv)
-    text_grad = trade_corners(text_part + to_mate(text_part))
+    text_grad = text_part + to_mate(text_part)
     back_two = scatter_pair(query_grad, lambda part: dot_last(part, w_query))
     rows_two, gain_two, shift_two = norm_back(after_self, 1, back_two)
     self_rows_grad = cross_rows_grad + rows_two
     self_grads = gather_pair(low(self_rows_grad))
-    self_out_grad = share_grad(dot_first(self_grads, self_mixed)).T
+    cross_out_grad, query_weight_grad, kv_weight_grad, self_out_grad = share_grads(
+        [
+            start_sums(cross_grads, cross_mixed),
+            start_sums(normed_two, query_grad),
+            start_sums(text_low, pair_grad),
+            start_sums(self_grads, self_mixed),
+        ]
+    )
     self_mixed_grad = low(dot(self_grads, w_self_out))
     triple_grad = fused_self_back(triple, self_logs, self_mixed_grad)
-    qkv_grad = share_grad(dot_first(normed_one, triple_grad)).reshape(depth, 3, lanes)
+    (qkv_grad,) = share_grads([start_sums(normed_one, triple_grad)])
     back_one = scatter_pair(triple_grad, lambda part: dot_last(part, w_qkv))
     rows_one, gain_one, shift_one = norm_back(rows, 0, back_one)
-    states_grad = trade_corners(self_rows_grad + rows_one)
-    norm_parts = jnp.stack([gain_one, gain_two, gain_three, shift_one, shift_two, shift_three])
-    norm_total = lax.psum(norm_parts, ("site", "core", "y"))
+    states_grad = trade_corners(low(self_rows_grad + rows_one)).astype(f32)
+    norm_total = sum_everywhere(
+        jnp.stack([gain_one, gain_two, gain_three, shift_one, shift_two, shift_three])
+    )
+    late = (layer_out, text_grad)
+    swapped = [lax.ppermute(part, ("core", "y"), [(1, 2), (2, 1)]) for part in late]
+    swapped = lax.optimization_barrier((*swapped, norm_total))[:2]
+    layer_out, text_grad = [
+        jnp.where(at_corner(), theirs, ours).astype(f32) for theirs, ours in zip(swapped, late)
+    ]
     width = norm_gains.shape[1]
-    place = lax.axis_index("site") * 2 + lax.axis_index("core")
+    place = (lax.axis_index("z") * 2 + lax.axis_index("x")) * 2 + lax.axis_index("core")
     norm_own = lax.dynamic_slice_in_dim(norm_total, place * width, width, 1)
     return (
         layer_out,
@@ -687,13 +777,13 @@
         text_grad[None],
         norm_own[:3],
         norm_own[3:],
-        qkv_grad,
-        self_out_grad,
+        qkv_grad.reshape(depth, 3, lanes),
+        self_out_grad.T,
         query_weight_grad,
-        kv_weight_grad,
-        cross_out_grad,
+        kv_weight_grad.reshape(depth, 2, lanes),
+        cross_out_grad.T,
         up_grad,
-        down_grad,
+        down_grad.T,
     )
 
 
@@ -716,10 +806,10 @@
 
 def solution(mesh):
     dp, tensor = mesh.shape["dp"], mesh.shape["tensor"]
-    if tensor == 2 and dp % 2 == 0:
+    if tensor == 2 and dp % 4 == 0 and dp & (dp - 1) == 0:
         body = on_pair
-        mesh = Mesh(mesh.devices.reshape(dp // 2, 2, 2), ("site", "core", "y"))
-        taken, given = placements(("site", "core"), ("y",))
+        mesh = Mesh(mesh.devices.reshape(dp // 4, 2, 2, 2), ("z", "x", "core", "y"))
+        taken, given = placements(("z", "x", "core"), ("y",))
     else:
         body = on_device
         taken, given = placements(("dp",), ("tensor",))

time: 1840 us -> 1280 us (0.70)
  waiting for transfers between devices: 1040 us -> 528 us
  local copies, waits for them, and re-layouts: 36.8 us -> 113 us
  starting transfers between devices: 160 us -> 103 us
  blocking collectives: 56.8 us -> 0 us
  other arithmetic: 52 us -> 103 us
  matrix products: 323 us -> 274 us
    reduce_scatter x6 -> x4, waiting for transfers between devices: 473 us -> 0.47 us  [share_grads(): summed = lax.psum_scatter(joined, 'z', scatter_dimension=0, tiled=True)[0]]
    ppermute x33 -> x82, waiting for transfers between devices: 214 us -> 466 us  [the longest x68 419 us: to_mate(): return lax.ppermute(values, axis, [(0, 1), (1, 0)])]
    all_gather x7 -> x4, waiting for transfers between devices: 255 us -> 61 us  [fetch(): line = lax.all_gather(shard, 'z', axis=0)]
    unnamed x15 -> x8, waiting for transfers between devices: 97.6 us -> 0.13 us
    ppermute x33 -> x82, starting transfers between devices: 149 us -> 102 us  [the longest x68 62.3 us: to_mate(): return lax.ppermute(values, axis, [(0, 1), (1, 0)])]
    dot_general x7, matrix products: 137 us -> 90.9 us  [dot(): return jnp.dot(left, right, preferred_element_type=f32)]
    psum x1 -> x0, blocking collectives: 39.1 us -> none  [on_pair(): norm_total = lax.psum(norm_parts, ('site', 'core', 'y'))]
    dynamic_update_slice x0 -> x24, local copies, waits for them, and re-layouts: none -> 36.8 us  [fetch(): lax.dynamic_update_slice(whole, piece.reshape(count, 1, 1, rows, width),...]
  transfers between devices with their start and end apart: 47 -> 90, of which waited for: 28 -> 39; matrix products, arithmetic and copies ran while one was open for 18% -> 29% of each run, Pallas kernels for 8% -> 11%
where the time goes in v2:
time: 1280 us
  waiting for transfers between devices  528 us (41%)
  matrix products  274 us (21%)
  Pallas kernels  139 us (11%)
  local copies, waits for them, and re-layouts  113 us (9%)
  starting transfers between devices  103 us (8%)
  other arithmetic  103 us (8%)
  between operations  16.8 us (1%)
    ppermute x68, waiting for transfers between devices, to_mate(): return lax.ppermute(values, axis, [(0, 1), (1, 0)])  419 us
    dot_general x13, matrix products, dot_last(): lax.dot_general(left, right, (((1,), (1,)), ((), ())), preferred_element_...  108 us
    dot_general x7, matrix products, dot(): return jnp.dot(left, right, preferred_element_type=f32)  90.9 us
    dot_general x14, matrix products, dot_first(): lax.dot_general(left, right, (((0,), (0,)), ((), ())), preferred_element_...  75.9 us
    pallas_call x1, Pallas kernels, fused_self_back(): pl.pallas_call(functools.partial(self_back_kernel, min(ROWS_STEP, length)...  74 us
    ppermute x68, starting transfers between devices, to_mate(): return lax.ppermute(values, axis, [(0, 1), (1, 0)])  62.3 us
    all_gather x4, waiting for transfers between devices, fetch(): line = lax.all_gather(shard, 'z', axis=0)  61 us
    pallas_call x2, Pallas kernels, fused_attend(): pl.pallas_call(functools.partial(attend_kernel, causal, block), grid=(pai...  45.6 us
  transfers between devices with their start and end apart: 90, of which 39 were waited for; matrix products, arithmetic and copies ran while one was open for 29% of the time, Pallas kernels for 11%

profile of v2, /device:TPU:1, one launch (start us, length us, event | category | flops | bytes accessed | tf_op | source)
XLA Modules:
  0.0 1276.5 jit_solution(17008905445473143243)
XLA Ops:
  11.9 4.5 collective-permute-start
  19.8 23.6 %collective-permute-done.2 = bf16[96,2560]{1,0:T(8,128)(2,1)S(1)} collective-permute-done((bf16[96,2560]{1,0:T(8,128)(2,1)S(1)}, bf16[96,2560]{1,0:T(8,128)(2,1)S(1)}, u32[]{:S(2)}, u32[]{:S(2)}) %collective-permute-start.2) | collective-permute-done | bytes 491552 | tf_op jit(solution)/shard_map/ppermute | solution.py:562
  51.1 37.9 %all-gather.9.cloned.1.call-done = bf16[384,2560]{1,0:T(8,128)(2,1)} async-done(((bf16[96,2560]{1,0:T(8,128)(2,1)}), bf16[384,2560]{1,0:T(8,128)(2,1)}) %all-gather.9.cloned.1.call-update) | async-done | bytes 1966096 | tf_op jit(solution)/shard_map/all_gather | solution.py:591
  94.7 20.1 %collective-permute-done.3 = bf16[384,1280]{1,0:T(8,128)(2,1)} collective-permute-done((bf16[384,1280]{1,0:T(8,128)(2,1)}, bf16[384,1280]{1,0:T(8,128)(2,1)}, u32[]{:S(2)}, u32[]{:S(2)}) %collective-permute-start.3) | collective-permute-done | bytes 983072 | tf_op jit(solution)/shard_map/ppermute | solution.py:567
  119.3 9.8 collective-permute-done.6
  133.3 16.9 %collective-permute-done.4 = bf16[384,1280]{1,0:T(8,128)(2,1)} collective-permute-done((bf16[384,1280]{1,0:T(8,128)(2,1)}, bf16[384,1280]{1,0:T(8,128)(2,1)}, u32[]{:S(2)}, u32[]{:S(2)}) %collective-permute-start.4) | collective-permute-done | bytes 983072 | tf_op jit(solution)/shard_map/ppermute | solution.py:567
  151.5 14.2 %collective-permute-done.5 = bf16[384,1280]{1,0:T(8,128)(2,1)} collective-permute-done((bf16[384,1280]{1,0:T(8,128)(2,1)}, bf16[384,1280]{1,0:T(8,128)(2,1)}, u32[]{:S(2)}, u32[]{:S(2)}) %collective-permute-start.5) | collective-permute-done | bytes 983072 | tf_op jit(solution)/shard_map/ppermute | solution.py:567
  186.1 28.6 %collective-permute-done.10 = bf16[384,1920]{1,0:T(8,128)(2,1)} collective-permute-done((bf16[384,1920]{1,0:T(8,128)(2,1)}, bf16[384,1920]{1,0:T(8,128)(2,1)}, u32[]{:S(2)}, u32[]{:S(2)}) %collective-permute-start.10) | collective-permute-done | bytes 1474592 | tf_op jit(solution)/shard_map/ppermute | solution.py:567
  217.1 7.3 broadcast_in_dim.23
  227.0 20.2 %collective-permute-done.11 = bf16[384,1920]{1,0:T(8,128)(2,1)} collective-permute-done((bf16[384,1920]{1,0:T(8,128)(2,1)}, bf16[384,1920]{1,0:T(8,128)(2,1)}, u32[]{:S(2)}, u32[]{:S(2)}) %collective-permute-start.11) | collective-permute-done | bytes 1474592 | tf_op jit(solution)/shard_map/ppermute | solution.py:567
  255.4 13.2 %convolution_convert_fusion.q_ref.k_ref.v_ref = bf16[1536,2304]{1,0:T(8,128)(2,1)} fusion(bf16[1536,2560]{1,0:T(8,128)(2,1)S(1)} %bitcast.344, bf16[768,1536]{1,0:T(8,128)(2,1)S(1)} %get-tuple-element.112, bf16[768,1536]{1,0:T(8,128)(2,1)S(1)} %get-tuple-element.111), kind=kOutput, calls=%fused_computation.9 | convolution fusion | flops 10884612096 | bytes 18874368 | tf_op jit(solution)/shard_map/dot_general | solution.py:709
  268.7 32.4 %attend_self.1 = (bf16[1536,768]{1,0:T(8,128)(2,1)}, f32[6,2,1536]{2,1,0:T(2,128)}) custom-call(bf16[1536,2304]{1,0:T(8,128)(2,1)} %convolution_convert_fusion.q_ref.k_ref.v_ref, bf16[1536,2304]{1,0:T(8,128)(2,1)} %convolution_convert_fusion.q_ref.k_ref.v_ref, bf16[1536,2304]{1,0:T(8,128)(2,1)} %convolution_convert_fusion.q_ref.k_ref.v_ref), custom_call_target="tpu_custom_call" | custom-call | flops 7247757312 | bytes 9437184 | tf_op jit(solution)/shard_map/attend_self/pallas_call | solution.py:476
  312.0 5.1 convolution_convert_fusion.14
  325.0 6.0 fusion.159
  346.6 21.3 %all-gather.13.cloned.1.call-done = bf16[384,3072]{1,0:T(8,128)(2,1)} async-done(((bf16[96,3072]{1,0:T(8,128)(2,1)}), bf16[384,3072]{1,0:T(8,128)(2,1)}) %all-gather.13.cloned.1.call-update) | async-done | bytes 2359312 | tf_op jit(solution)/shard_map/all_gather | solution.py:591
  386.3 8.2 convolution_convert_fusion.13.q_ref
  394.5 13.1 %attend_cross.1 = (bf16[1536,768]{1,0:T(8,128)(2,1)}, f32[6,2,1536]{2,1,0:T(2,128)}) custom-call(bf16[1536,768]{1,0:T(8,128)(2,1)} %convolution_convert_fusion.13.q_ref, bf16[64,1536]{1,0:T(8,128)(2,1)} %fusion.60.k_ref.v_ref, bf16[64,1536]{1,0:T(8,128)(2,1)} %fusion.60.k_ref.v_ref), custom_call_target="tpu_custom_call" | custom-call | flops 301989888 | bytes 4915200 | tf_op jit(solution)/shard_map/attend_cross/pallas_call | solution.py:476
  407.7 5.5 convolution_convert_fusion.12
  414.7 6.4 broadcast_in_dim.24
  426.2 4.8 broadcast_in_dim.25
  436.2 22.0 %collective-permute-done.23 = bf16[384,1536]{1,0:T(8,128)(2,1)S(1)} collective-permute-done((bf16[384,1536]{1,0:T(8,128)(2,1)}, bf16[384,1536]{1,0:T(8,128)(2,1)S(1)}, u32[]{:S(2)}, u32[]{:S(2)}) %collective-permute-start.23) | collective-permute-done | bytes 1179680 | tf_op jit(solution)/shard_map/ppermute | solution.py:567
  461.5 22.0 %collective-permute-done.24 = bf16[384,1536]{1,0:T(8,128)(2,1)S(1)} collective-permute-done((bf16[384,1536]{1,0:T(8,128)(2,1)}, bf16[384,1536]{1,0:T(8,128)(2,1)S(1)}, u32[]{:S(2)}, u32[]{:S(2)}) %collective-permute-start.24) | collective-permute-done | bytes 1179680 | tf_op jit(solution)/shard_map/ppermute | solution.py:567
  489.8 5.4 fusion.160
  497.2 11.6 collective-permute-done.30
  515.3 9.7 collective-permute-done.29
  527.3 11.2 collective-permute-done.31
  539.7 24.1 %collective-permute-done.32 = bf16[384,1536]{1,0:T(8,128)(2,1)S(1)} collective-permute-done((bf16[384,1536]{1,0:T(8,128)(2,1)S(1)}, bf16[384,1536]{1,0:T(8,128)(2,1)S(1)}, u32[]{:S(2)}, u32[]{:S(2)}) %collective-permute-start.32) | collective-permute-done | bytes 1179680 | tf_op jit(solution)/shard_map/ppermute | solution.py:567
  567.0 21.1 %multiply_convert_fusion.1 = (bf16[1536,3072]{1,0:T(8,128)(2,1)}, f32[1536,3072]{1,0:T(8,128)}) fusion(bf16[1536,3072]{1,0:T(8,128)(2,1)S(1)} %bitcast.324, bf16[768,1536]{1,0:T(8,128)(2,1)S(1)} %get-tuple-element.108, bf16[768,1536]{1,0:T(8,128)(2,1)S(1)} %get-tuple-element.107), kind=kOutput, calls=%fused_computation.7 | convolution fusion | flops 14528544768 | bytes 42467328 | tf_op jit(solution)/shard_map/dot_general | solution.py:709
  588.0 27.8 %multiply_convert_fusion = bf16[1536,3072]{1,0:T(8,128)(2,1)} fusion(bf16[1536,3072]{1,0:T(8,128)(2,1)} %bitcast.327, f32[1536,3072]{1,0:T(8,128)} %get-tuple-element.144, bf16[768,1536]{1,0:T(8,128)(2,1)S(1)} %get-tuple-element.106, bf16[768,1536]{1,0:T(8,128)(2,1)S(1)} %get-tuple-element.105), kind=kOutput, calls=%fused_computation.6 | convolution fusion | flops 14561574912 | bytes 42467328 | tf_op jit(solution)/shard_map/dot_general | solution.py:709
  615.8 10.5 fusion.43
  626.3 9.7 convolution_convert_fusion.5
  636.0 10.5 convolution_convert_fusion.6
  646.6 10.9 fusion.40
  657.5 9.9 convolution_convert_fusion.4
  676.5 9.7 convolution_convert_fusion.3
  689.0 34.0 %collective-permute-done.72 = bf16[768,1536]{1,0:T(8,128)(2,1)S(1)} collective-permute-done((bf16[768,1536]{1,0:T(8,128)(2,1)S(1)}, bf16[768,1536]{1,0:T(8,128)(2,1)S(1)}, u32[]{:S(2)}, u32[]{:S(2)}) %collective-permute-start.72) | collective-permute-done | bytes 2359328 | tf_op jit(solution)/shard_map/ppermute | solution.py:567
  726.3 13.0 %multiply_reduce_fusion.1 = (f32[1536]{0:T(1024)S(1)}, f32[768]{0:T(1024)S(1)}, f32[1536]{0:T(1024)S(1)}, f32[768,1536]{1,0:T(8,128)S(1)}) fusion(f32[768,1536]{1,0:T(8,128)S(1)} %bitcast.306, f32[768]{0:T(1024)S(1)} %copy-done.79, f32[768]{0:T(1024)S(1)} %copy-done.68, f32[1536]{0:T(1024)S(1)} %copy-done.62, ...), kind=kOutput, calls=%fused_computation.44 | convolution fusion | flops 7259550208 | bytes 25979908 | tf_op jit(solution)/shard_map/dot_general | solution.py:307
  748.0 52.0 %collective-permute-done.73 = bf16[384,1536]{1,0:T(8,128)(2,1)} collective-permute-done((bf16[384,1536]{1,0:T(8,128)(2,1)}, bf16[384,1536]{1,0:T(8,128)(2,1)}, u32[]{:S(2)}, u32[]{:S(2)}) %collective-permute-start.73) | collective-permute-done | bytes 1179680 | tf_op jit(solution)/shard_map/ppermute | solution.py:567
  814.1 13.1 %add_convert_fusion.1 = bf16[768,1536]{1,0:T(8,128)(2,1)} fusion(f32[768,1536]{1,0:T(8,128)S(1)} %bitcast.308, bf16[768,1536]{1,0:T(8,128)(2,1)} %collective-permute-done.33, bf16[1536,3072]{1,0:T(8,128)(2,1)} %bitcast.328, bf16[1536,3072]{1,0:T(8,128)(2,1)} %get-tuple-element.143, s32[]{:T(128)S(6)} %select_n.286), kind=kOutput, calls=%fused_computation.58 | convolution fusion | flops 7252475904 | bytes 23592964 | tf_op jit(solution)/shard_map/dot_general | solution.py:307
  831.5 5.4 collective-permute-done.78
  852.9 8.4 convolution_convert_fusion.11.grad_ref
  861.3 19.3 %attend_cross_back.1 = (bf16[1536,768]{1,0:T(8,128)(2,1)}, bf16[64,768]{1,0:T(8,128)(2,1)}, bf16[64,768]{1,0:T(8,128)(2,1)}) custom-call(bf16[1536,768]{1,0:T(8,128)(2,1)} %convolution_convert_fusion.13.q_ref, bf16[64,1536]{1,0:T(8,128)(2,1)} %fusion.60.k_ref.v_ref, bf16[64,1536]{1,0:T(8,128)(2,1)} %fusion.60.k_ref.v_ref, ...), custom_call_target="tpu_custom_call" | custom-call | flops 754974720 | bytes 12288000 | tf_op jit(solution)/shard_map/attend_cross_back/pallas_call | solution.py:530
  880.7 4.2 convolution_convert_fusion.10
  886.2 4.8 fusion.26
  903.5 5.4 multiply_reduce_fusion.2
  923.2 8.2 collective-permute-done.59
  934.9 6.2 collective-permute-done.56
  942.5 20.5 %collective-permute-done.58 = bf16[384,384]{1,0:T(8,128)(2,1)S(1)} collective-permute-done((bf16[384,384]{1,0:T(8,128)(2,1)S(1)}, bf16[384,384]{1,0:T(8,128)(2,1)S(1)}, u32[]{:S(2)}, u32[]{:S(2)}) %collective-permute-start.58) | collective-permute-done | bytes 294944 | tf_op jit(solution)/shard_map/ppermute | solution.py:567
  967.8 8.2 convolution_convert_fusion.9.grad_ref
  976.1 74.0 %attend_self_back.1 = bf16[1536,2304]{1,0:T(8,128)(2,1)} custom-call(bf16[1536,2304]{1,0:T(8,128)(2,1)} %convolution_convert_fusion.q_ref.k_ref.v_ref, bf16[1536,2304]{1,0:T(8,128)(2,1)} %convolution_convert_fusion.q_ref.k_ref.v_ref, bf16[1536,2304]{1,0:T(8,128)(2,1)} %convolution_convert_fusion.q_ref.k_ref.v_ref, ...), custom_call_target="tpu_custom_call" | custom-call | flops 18119393280 | bytes 23592960 | tf_op jit(solution)/shard_map/attend_self_back/pallas_call | solution.py:507
  1050.1 9.9 convolution_convert_fusion.2
  1061.7 6.6 convolution_convert_fusion.1
  1071.5 4.4 collective-permute-start.40
  1081.0 18.0 %collective-permute-done.50 = bf16[768,1152]{1,0:T(8,128)(2,1)S(1)} collective-permute-done((bf16[768,1152]{1,0:T(8,128)(2,1)S(1)}, bf16[768,1152]{1,0:T(8,128)(2,1)S(1)}, u32[]{:S(2)}, u32[]{:S(2)}) %collective-permute-start.50) | collective-permute-done | bytes 1769504 | tf_op jit(solution)/shard_map/ppermute | solution.py:567
  1100.6 6.6 collective-permute-done.52
  1113.9 30.1 %collective-permute-done.51 = bf16[384,1152]{1,0:T(8,128)(2,1)S(1)} collective-permute-done((bf16[384,1152]{1,0:T(8,128)(2,1)S(1)}, bf16[384,1152]{1,0:T(8,128)(2,1)S(1)}, u32[]{:S(2)}, u32[]{:S(2)}) %collective-permute-start.51) | collective-permute-done | bytes 884768 | tf_op jit(solution)/shard_map/ppermute | solution.py:567
  1147.0 10.1 fusion.46
  1167.4 10.0 collective-permute-done.69
  1195.0 13.4 %multiply_reduce_fusion = (f32[768]{0:T(1024)S(1)}, f32[1536]{0:T(1024)S(1)}, f32[1536]{0:T(1024)S(1)}, f32[768,1536]{1,0:T(8,128)}) fusion(f32[768,1536]{1,0:T(8,128)} %copy-done, f32[1536]{0:T(1024)S(1)} %copy-done.58, f32[768]{0:T(1024)S(1)} %copy-done.64, f32[768]{0:T(1024)S(1)} %copy-done.75, bf16[768,1536]{1,0:T(8,128)(2,1)} %collective-permute-done.43, ...), kind=kOutput, calls=%fused_computation.43 | convolution fusion | flops 5447610368 | bytes 22440964 | tf_op jit(solution)/shard_map/dot_general | solution.py:307
  1208.7 4.6 fusion.149
  1218.4 5.7 add_convert_fusion
  1229.7 4.4 collective-permute-done.47
  1235.3 7.2 collective-permute-done.48
  1260.3 6.8 collective-permute-done.71
  (602 shorter events, 329.6 us)
Async XLA Ops:
  7.2 81.8 %all-gather.9.cloned.1.call-start = ((), (), s32[]{:S(2)}) async-start(), calls=%async_computation.8 | async-start | bytes 2457600 | tf_op jit(solution)/shard_map/all_gather | solution.py:591
  11.9 32.5 %collective-permute-start = (bf16[96,9984]{1,0:T(8,128)(2,1)S(1)}, bf16[96,9984]{1,0:T(8,128)(2,1)}, u32[]{:S(2)}, u32[]{:S(2)}) collective-permute-start(bf16[96,9984]{1,0:T(8,128)(2,1)S(1)} %bitcast_dynamic-update-slice_fusion), channel_id=1, source_target_pairs={{1,2},{2,1},{5,6},{6,5},{9,10},{10,9},{13,14},{14,13},{17,18},{18,... | collective-permute-start | bytes 5750792 | tf_op jit(solution)/shard_map/ppermute | solution.py:562
  44.4 133.4 %all-gather.11.cloned.1.call-start = ((), (), s32[]{:S(2)}) async-start(), calls=%async_computation.9 | async-start | bytes 3686400 | tf_op jit(solution)/shard_map/all_gather | solution.py:591
  47.4 122.4 %collective-permute-start.1 = (f32[768,1536]{1,0:T(8,128)}, f32[768,1536]{1,0:T(8,128)}, u32[]{:S(2)}, u32[]{:S(2)}) collective-permute-start(f32[768,1536]{1,0:T(8,128)} %param.12), channel_id=1, source_target_pairs={{1,2},{2,1},{5,6},{6,5},{9,10},{10,9},{13,14},{14,13},{17,18},{18,... | collective-permute-start | bytes 14155784 | tf_op jit(solution)/shard_map/ppermute | solution.py:562
  93.2 35.9 %collective-permute-start.6 = (bf16[384,1280]{1,0:T(8,128)(2,1)}, bf16[384,1280]{1,0:T(8,128)(2,1)S(1)}, u32[]{:S(2)}, u32[]{:S(2)}) collective-permute-start(bf16[384,1280]{1,0:T(8,128)(2,1)} %bitcast.9), channel_id=1, source_target_pairs={{0,1},{1,0},{2,3},{3,2},{4,5},{5,4},{6,7},{7,6},{8,9},{9,8},{10,11... | collective-permute-start | bytes 2949128 | tf_op jit(solution)/shard_map/ppermute | solution.py:567
  94.4 55.8 %collective-permute-start.4 = (bf16[384,1280]{1,0:T(8,128)(2,1)}, bf16[384,1280]{1,0:T(8,128)(2,1)}, u32[]{:S(2)}, u32[]{:S(2)}) collective-permute-start(bf16[384,1280]{1,0:T(8,128)(2,1)} %bitcast.5), channel_id=1, source_target_pairs={{0,1},{1,0},{2,3},{3,2},{4,5},{5,4},{6,7},{7,6},{8,9},{9,8},{10,11... | collective-permute-start | bytes 2949128 | tf_op jit(solution)/shard_map/ppermute | solution.py:567
  114.7 50.9 %collective-permute-start.5 = (bf16[384,1280]{1,0:T(8,128)(2,1)}, bf16[384,1280]{1,0:T(8,128)(2,1)}, u32[]{:S(2)}, u32[]{:S(2)}) collective-permute-start(bf16[384,1280]{1,0:T(8,128)(2,1)} %collective-permute-done.3), channel_id=1, source_target_pairs={{0,1},{1,0},{2,3},{3,2},{4,5},{5,4},{6,7},{7,6},{8,9},{9,8},{10,11... | collective-permute-start | bytes 2949128 | tf_op jit(solution)/shard_map/ppermute | solution.py:567
  118.0 225.0 %all-gather.15.cloned.1.call-start = ((), (), s32[]{:S(2)}) async-start(), calls=%async_computation.11 | async-start | bytes 2949120 | tf_op jit(solution)/shard_map/all_gather | solution.py:591
  118.0 49.1 %collective-permute-start.7 = (bf16[384,1280]{1,0:T(8,128)(2,1)}, bf16[384,1280]{1,0:T(8,128)(2,1)S(1)}, u32[]{:S(2)}, u32[]{:S(2)}) collective-permute-start(bf16[384,1280]{1,0:T(8,128)(2,1)} %bitcast.9), channel_id=1, source_target_pairs={{0,4},{4,0},{1,5},{5,1},{2,6},{6,2},{3,7},{7,3},{8,12},{12,8},{9,1... | collective-permute-start | bytes 2949128 | tf_op jit(solution)/shard_map/ppermute | solution.py:567
  129.1 38.2 %collective-permute-start.8 = (bf16[384,1280]{1,0:T(8,128)(2,1)S(1)}, bf16[384,1280]{1,0:T(8,128)(2,1)S(1)}, u32[]{:S(2)}, u32[]{:S(2)}) collective-permute-start(bf16[384,1280]{1,0:T(8,128)(2,1)S(1)} %collective-permute-done.6), channel_id=1, source_target_pairs={{0,4},{4,0},{1,5},{5,1},{2,6},{6,2},{3,7},{7,3},{8,12},{12,8},{9,1... | collective-permute-start | bytes 2949128 | tf_op jit(solution)/shard_map/ppermute | solution.py:567
  176.0 74.0 %collective-permute-start.9 = (bf16[768,1536]{1,0:T(8,128)(2,1)}, bf16[768,1536]{1,0:T(8,128)(2,1)}, u32[]{:S(2)}, u32[]{:S(2)}) collective-permute-start(bf16[768,1536]{1,0:T(8,128)(2,1)} %add_convert_fusion.4), channel_id=1, source_target_pairs={{0,2},{2,0},{1,3},{3,1},{4,6},{6,4},{5,7},{7,5},{8,10},{10,8},{9,1... | collective-permute-start | bytes 7077896 | tf_op jit(solution)/shard_map/ppermute | solution.py:567
  181.4 33.3 %collective-permute-start.10 = (bf16[384,1920]{1,0:T(8,128)(2,1)}, bf16[384,1920]{1,0:T(8,128)(2,1)}, u32[]{:S(2)}, u32[]{:S(2)}) collective-permute-start(bf16[384,1920]{1,0:T(8,128)(2,1)} %bitcast.16), channel_id=1, source_target_pairs={{0,4},{4,0},{1,5},{5,1},{2,6},{6,2},{3,7},{7,3},{8,12},{12,8},{9,1... | collective-permute-start | bytes 4423688 | tf_op jit(solution)/shard_map/ppermute | solution.py:567
  182.5 33.3 %collective-permute-start.13 = (bf16[384,1920]{1,0:T(8,128)(2,1)}, bf16[384,1920]{1,0:T(8,128)(2,1)}, u32[]{:S(2)}, u32[]{:S(2)}) collective-permute-start(bf16[384,1920]{1,0:T(8,128)(2,1)} %bitcast.20), channel_id=1, source_target_pairs={{0,1},{1,0},{2,3},{3,2},{4,5},{5,4},{6,7},{7,6},{8,9},{9,8},{10,11... | collective-permute-start | bytes 4423688 | tf_op jit(solution)/shard_map/ppermute | solution.py:567
  183.7 63.4 %collective-permute-start.11 = (bf16[384,1920]{1,0:T(8,128)(2,1)}, bf16[384,1920]{1,0:T(8,128)(2,1)}, u32[]{:S(2)}, u32[]{:S(2)}) collective-permute-start(bf16[384,1920]{1,0:T(8,128)(2,1)} %bitcast.16), channel_id=1, source_target_pairs={{0,1},{1,0},{2,3},{3,2},{4,5},{5,4},{6,7},{7,6},{8,9},{9,8},{10,11... | collective-permute-start | bytes 4423688 | tf_op jit(solution)/shard_map/ppermute | solution.py:567
  185.2 182.7 %all-gather.13.cloned.1.call-start = ((), (), s32[]{:S(2)}) async-start(), calls=%async_computation.10 | async-start | bytes 2949120 | tf_op jit(solution)/shard_map/all_gather | solution.py:591
  185.8 120.7 %collective-permute-start.14 = (bf16[384,1920]{1,0:T(8,128)(2,1)}, bf16[384,1920]{1,0:T(8,128)(2,1)}, u32[]{:S(2)}, u32[]{:S(2)}) collective-permute-start(bf16[384,1920]{1,0:T(8,128)(2,1)} %bitcast.20), channel_id=1, source_target_pairs={{0,4},{4,0},{1,5},{5,1},{2,6},{6,2},{3,7},{7,3},{8,12},{12,8},{9,1... | collective-permute-start | bytes 4423688 | tf_op jit(solution)/shard_map/ppermute | solution.py:567
  214.7 86.4 %collective-permute-start.12 = (bf16[384,1920]{1,0:T(8,128)(2,1)}, bf16[384,1920]{1,0:T(8,128)(2,1)}, u32[]{:S(2)}, u32[]{:S(2)}) collective-permute-start(bf16[384,1920]{1,0:T(8,128)(2,1)} %collective-permute-done.10), channel_id=1, source_target_pairs={{0,1},{1,0},{2,3},{3,2},{4,5},{5,4},{6,7},{7,6},{8,9},{9,8},{10,11... | collective-permute-start | bytes 4423688 | tf_op jit(solution)/shard_map/ppermute | solution.py:567
  215.9 93.5 %collective-permute-start.15 = (bf16[384,1920]{1,0:T(8,128)(2,1)}, bf16[384,1920]{1,0:T(8,128)(2,1)}, u32[]{:S(2)}, u32[]{:S(2)}) collective-permute-start(bf16[384,1920]{1,0:T(8,128)(2,1)} %collective-permute-done.13), channel_id=1, source_target_pairs={{0,4},{4,0},{1,5},{5,1},{2,6},{6,2},{3,7},{7,3},{8,12},{12,8},{9,1... | collective-permute-start | bytes 4423688 | tf_op jit(solution)/shard_map/ppermute | solution.py:567
  320.7 860.9 %reduce-scatter.9.cloned.1.call-start = ((), (), s32[]{:S(2)}) async-start(), calls=%async_computation.6 | async-start | bytes 2949120 | tf_op jit(solution)/shard_map/reduce_scatter | solution.py:634
  334.6 43.1 %collective-permute-start.17 = (bf16[768,1536]{1,0:T(8,128)(2,1)}, bf16[768,1536]{1,0:T(8,128)(2,1)}, u32[]{:S(2)}, u32[]{:S(2)}) collective-permute-start(bf16[768,1536]{1,0:T(8,128)(2,1)} %add_convert_fusion.3), channel_id=1, source_target_pairs={{0,2},{2,0},{1,3},{3,1},{4,6},{6,4},{5,7},{7,5},{8,10},{10,8},{9,1... | collective-permute-start | bytes 7077896 | tf_op jit(solution)/shard_map/ppermute | solution.py:567
  346.3 87.3 %collective-permute-start.28 = (bf16[384,1536]{1,0:T(8,128)(2,1)}, bf16[384,1536]{1,0:T(8,128)(2,1)}, u32[]{:S(2)}, u32[]{:S(2)}) collective-permute-start(bf16[384,1536]{1,0:T(8,128)(2,1)} %bitcast.37), channel_id=1, source_target_pairs={{0,1},{1,0},{2,3},{3,2},{4,5},{5,4},{6,7},{7,6},{8,9},{9,8},{10,11... | collective-permute-start | bytes 3538952 | tf_op jit(solution)/shard_map/ppermute | solution.py:567
  346.3 66.9 %collective-permute-start.27 = (bf16[384,1536]{1,0:T(8,128)(2,1)}, bf16[384,1536]{1,0:T(8,128)(2,1)}, u32[]{:S(2)}, u32[]{:S(2)}) collective-permute-start(bf16[384,1536]{1,0:T(8,128)(2,1)} %bitcast.37), channel_id=1, source_target_pairs={{0,4},{4,0},{1,5},{5,1},{2,6},{6,2},{3,7},{7,3},{8,12},{12,8},{9,1... | collective-permute-start | bytes 3538952 | tf_op jit(solution)/shard_map/ppermute | solution.py:567
  371.3 42.1 %collective-permute-start.22 = (bf16[384,1536]{1,0:T(8,128)(2,1)}, bf16[384,1536]{1,0:T(8,128)(2,1)}, u32[]{:S(2)}, u32[]{:S(2)}) collective-permute-start(bf16[384,1536]{1,0:T(8,128)(2,1)} %bitcast.27), channel_id=1, source_target_pairs={{0,1},{1,0},{2,3},{3,2},{4,5},{5,4},{6,7},{7,6},{8,9},{9,8},{10,11... | collective-permute-start | bytes 3538952 | tf_op jit(solution)/shard_map/ppermute | solution.py:567
  372.5 40.6 %collective-permute-start.21 = (bf16[384,1536]{1,0:T(8,128)(2,1)}, bf16[384,1536]{1,0:T(8,128)(2,1)}, u32[]{:S(2)}, u32[]{:S(2)}) collective-permute-start(bf16[384,1536]{1,0:T(8,128)(2,1)} %bitcast.27), channel_id=1, source_target_pairs={{0,4},{4,0},{1,5},{5,1},{2,6},{6,2},{3,7},{7,3},{8,12},{12,8},{9,1... | collective-permute-start | bytes 3538952 | tf_op jit(solution)/shard_map/ppermute | solution.py:567
  377.7 108.0 %collective-permute-start.35 = (bf16[768,1536]{1,0:T(8,128)(2,1)S(1)}, bf16[768,1536]{1,0:T(8,128)(2,1)}, u32[]{:S(2)}, u32[]{:S(2)}) collective-permute-start(bf16[768,1536]{1,0:T(8,128)(2,1)S(1)} %convert_element_type.627), channel_id=1, source_target_pairs={{1,2},{2,1},{5,6},{6,5},{9,10},{10,9},{13,14},{14,13},{17,18},{18,... | collective-permute-start | bytes 7077896 | tf_op jit(solution)/shard_map/ppermute | solution.py:562
  413.1 76.5 %collective-permute-start.19 = (bf16[768,1536]{1,0:T(8,128)(2,1)}, bf16[768,1536]{1,0:T(8,128)(2,1)}, u32[]{:S(2)}, u32[]{:S(2)}) collective-permute-start(bf16[768,1536]{1,0:T(8,128)(2,1)} %convolution_convert_fusion.12), channel_id=1, source_target_pairs={{0,2},{2,0},{1,3},{3,1},{4,6},{6,4},{5,7},{7,5},{8,10},{10,8},{9,1... | collective-permute-start | bytes 7077896 | tf_op jit(solution)/shard_map/ppermute | solution.py:567
  413.2 45.1 %collective-permute-start.23 = (bf16[384,1536]{1,0:T(8,128)(2,1)}, bf16[384,1536]{1,0:T(8,128)(2,1)S(1)}, u32[]{:S(2)}, u32[]{:S(2)}) collective-permute-start(bf16[384,1536]{1,0:T(8,128)(2,1)} %collective-permute-done.21), channel_id=1, source_target_pairs={{0,1},{1,0},{2,3},{3,2},{4,5},{5,4},{6,7},{7,6},{8,9},{9,8},{10,11... | collective-permute-start | bytes 3538952 | tf_op jit(solution)/shard_map/ppermute | solution.py:567
  413.5 70.1 %collective-permute-start.24 = (bf16[384,1536]{1,0:T(8,128)(2,1)}, bf16[384,1536]{1,0:T(8,128)(2,1)S(1)}, u32[]{:S(2)}, u32[]{:S(2)}) collective-permute-start(bf16[384,1536]{1,0:T(8,128)(2,1)} %bitcast.31), channel_id=1, source_target_pairs={{0,1},{1,0},{2,3},{3,2},{4,5},{5,4},{6,7},{7,6},{8,9},{9,8},{10,11... | collective-permute-start | bytes 3538952 | tf_op jit(solution)/shard_map/ppermute | solution.py:567
  433.6 77.2 %collective-permute-start.25 = (bf16[384,1536]{1,0:T(8,128)(2,1)}, bf16[384,1536]{1,0:T(8,128)(2,1)S(1)}, u32[]{:S(2)}, u32[]{:S(2)}) collective-permute-start(bf16[384,1536]{1,0:T(8,128)(2,1)} %bitcast.31), channel_id=1, source_target_pairs={{0,4},{4,0},{1,5},{5,1},{2,6},{6,2},{3,7},{7,3},{8,12},{12,8},{9,1... | collective-permute-start | bytes 3538952 | tf_op jit(solution)/shard_map/ppermute | solution.py:567
  458.3 50.5 %collective-permute-start.30 = (bf16[384,1536]{1,0:T(8,128)(2,1)S(1)}, bf16[384,1536]{1,0:T(8,128)(2,1)S(1)}, u32[]{:S(2)}, u32[]{:S(2)}) collective-permute-start(bf16[384,1536]{1,0:T(8,128)(2,1)S(1)} %bitcast.391), channel_id=1, source_target_pairs={{0,1},{1,0},{2,3},{3,2},{4,5},{5,4},{6,7},{7,6},{8,9},{9,8},{10,11... | collective-permute-start | bytes 3538952 | tf_op jit(solution)/shard_map/ppermute | solution.py:567
  483.5 41.5 %collective-permute-start.29 = (bf16[384,1536]{1,0:T(8,128)(2,1)}, bf16[384,1536]{1,0:T(8,128)(2,1)S(1)}, u32[]{:S(2)}, u32[]{:S(2)}) collective-permute-start(bf16[384,1536]{1,0:T(8,128)(2,1)} %collective-permute-done.27), channel_id=1, source_target_pairs={{0,1},{1,0},{2,3},{3,2},{4,5},{5,4},{6,7},{7,6},{8,9},{9,8},{10,11... | collective-permute-start | bytes 3538952 | tf_op jit(solution)/shard_map/ppermute | solution.py:567
  489.7 75.2 %collective-permute-start.36 = (bf16[768,1536]{1,0:T(8,128)(2,1)S(1)}, bf16[768,1536]{1,0:T(8,128)(2,1)S(1)}, u32[]{:S(2)}, u32[]{:S(2)}) collective-permute-start(bf16[768,1536]{1,0:T(8,128)(2,1)S(1)} %broadcast_select_fusion.12), channel_id=1, source_target_pairs={{0,2},{2,0},{1,3},{3,1},{4,6},{6,4},{5,7},{7,5},{8,10},{10,8},{9,1... | collective-permute-start | bytes 7077896 | tf_op jit(solution)/shard_map/ppermute | solution.py:567
  508.7 29.8 %collective-permute-start.31 = (bf16[384,1536]{1,0:T(8,128)(2,1)S(1)}, bf16[384,1536]{1,0:T(8,128)(2,1)S(1)}, u32[]{:S(2)}, u32[]{:S(2)}) collective-permute-start(bf16[384,1536]{1,0:T(8,128)(2,1)S(1)} %bitcast.392), channel_id=1, source_target_pairs={{0,4},{4,0},{1,5},{5,1},{2,6},{6,2},{3,7},{7,3},{8,12},{12,8},{9,1... | collective-permute-start | bytes 3538952 | tf_op jit(solution)/shard_map/ppermute | solution.py:567
  510.8 54.4 %collective-permute-start.20 = (bf16[768,1536]{1,0:T(8,128)(2,1)S(1)}, bf16[768,1536]{1,0:T(8,128)(2,1)S(1)}, u32[]{:S(2)}, u32[]{:S(2)}) collective-permute-start(bf16[768,1536]{1,0:T(8,128)(2,1)S(1)} %add_convert_fusion.2), channel_id=1, source_target_pairs={{0,2},{2,0},{1,3},{3,1},{4,6},{6,4},{5,7},{7,5},{8,10},{10,8},{9,1... | collective-permute-start | bytes 7077896 | tf_op jit(solution)/shard_map/ppermute | solution.py:567
  513.2 50.5 %collective-permute-start.32 = (bf16[384,1536]{1,0:T(8,128)(2,1)S(1)}, bf16[384,1536]{1,0:T(8,128)(2,1)S(1)}, u32[]{:S(2)}, u32[]{:S(2)}) collective-permute-start(bf16[384,1536]{1,0:T(8,128)(2,1)S(1)} %collective-permute-done.30), channel_id=1, source_target_pairs={{0,4},{4,0},{1,5},{5,1},{2,6},{6,2},{3,7},{7,3},{8,12},{12,8},{9,1... | collective-permute-start | bytes 3538952 | tf_op jit(solution)/shard_map/ppermute | solution.py:567
  667.4 146.7 %collective-permute-start.33 = (bf16[768,1536]{1,0:T(8,128)(2,1)}, bf16[768,1536]{1,0:T(8,128)(2,1)}, u32[]{:S(2)}, u32[]{:S(2)}) collective-permute-start(bf16[768,1536]{1,0:T(8,128)(2,1)} %fusion.40), channel_id=1, source_target_pairs={{0,2},{2,0},{1,3},{3,1},{4,6},{6,4},{5,7},{7,5},{8,10},{10,8},{9,1... | collective-permute-start | bytes 7077896 | tf_op jit(solution)/shard_map/ppermute | solution.py:567
  667.9 57.4 %collective-permute-start.37 = (bf16[768,1536]{1,0:T(8,128)(2,1)S(1)}, bf16[768,1536]{1,0:T(8,128)(2,1)}, u32[]{:S(2)}, u32[]{:S(2)}) collective-permute-start(bf16[768,1536]{1,0:T(8,128)(2,1)S(1)} %copy-done.98), channel_id=1, source_target_pairs={{0,2},{2,0},{1,3},{3,1},{4,6},{6,4},{5,7},{7,5},{8,10},{10,8},{9,1... | collective-permute-start | bytes 7077896 | tf_op jit(solution)/shard_map/ppermute | solution.py:567
  669.8 53.2 %collective-permute-start.72 = (bf16[768,1536]{1,0:T(8,128)(2,1)S(1)}, bf16[768,1536]{1,0:T(8,128)(2,1)S(1)}, u32[]{:S(2)}, u32[]{:S(2)}) collective-permute-start(bf16[768,1536]{1,0:T(8,128)(2,1)S(1)} %bitcast.363), channel_id=1, source_target_pairs={{0,4},{4,0},{1,5},{5,1},{2,6},{6,2},{3,7},{7,3},{8,12},{12,8},{9,1... | collective-permute-start | bytes 7077896 | tf_op jit(solution)/shard_map/ppermute | solution.py:567
  671.6 67.6 %collective-permute-start.74 = (bf16[768,1536]{1,0:T(8,128)(2,1)}, bf16[768,1536]{1,0:T(8,128)(2,1)}, u32[]{:S(2)}, u32[]{:S(2)}) collective-permute-start(bf16[768,1536]{1,0:T(8,128)(2,1)} %bitcast.130), channel_id=1, source_target_pairs={{0,1},{1,0},{2,3},{3,2},{4,5},{5,4},{6,7},{7,6},{8,9},{9,8},{10,11... | collective-permute-start | bytes 7077896 | tf_op jit(solution)/shard_map/ppermute | solution.py:567
  675.2 130.8 %collective-permute-start.77 = (bf16[768,1536]{1,0:T(8,128)(2,1)}, bf16[768,1536]{1,0:T(8,128)(2,1)}, u32[]{:S(2)}, u32[]{:S(2)}) collective-permute-start(bf16[768,1536]{1,0:T(8,128)(2,1)} %bitcast.138), channel_id=1, source_target_pairs={{0,4},{4,0},{1,5},{5,1},{2,6},{6,2},{3,7},{7,3},{8,12},{12,8},{9,1... | collective-permute-start | bytes 7077896 | tf_op jit(solution)/shard_map/ppermute | solution.py:567
  723.0 86.8 %collective-permute-start.79 = (bf16[768,1536]{1,0:T(8,128)(2,1)}, bf16[768,1536]{1,0:T(8,128)(2,1)}, u32[]{:S(2)}, u32[]{:S(2)}) collective-permute-start(bf16[768,1536]{1,0:T(8,128)(2,1)} %bitcast.145), channel_id=1, source_target_pairs={{0,1},{1,0},{2,3},{3,2},{4,5},{5,4},{6,7},{7,6},{8,9},{9,8},{10,11... | collective-permute-start | bytes 7077896 | tf_op jit(solution)/shard_map/ppermute | solution.py:567
  725.3 74.6 %collective-permute-start.73 = (bf16[384,1536]{1,0:T(8,128)(2,1)}, bf16[384,1536]{1,0:T(8,128)(2,1)}, u32[]{:S(2)}, u32[]{:S(2)}) collective-permute-start(bf16[384,1536]{1,0:T(8,128)(2,1)} %bitcast.126), channel_id=1, source_target_pairs={{0,1},{1,0},{2,3},{3,2},{4,5},{5,4},{6,7},{7,6},{8,9},{9,8},{10,11... | collective-permute-start | bytes 3538952 | tf_op jit(solution)/shard_map/ppermute | solution.py:567
  741.7 62.1 %collective-permute-start.75 = (bf16[384,1536]{1,0:T(8,128)(2,1)S(1)}, bf16[384,1536]{1,0:T(8,128)(2,1)S(1)}, u32[]{:S(2)}, u32[]{:S(2)}) collective-permute-start(bf16[384,1536]{1,0:T(8,128)(2,1)S(1)} %bitcast.370), channel_id=1, source_target_pairs={{0,4},{4,0},{1,5},{5,1},{2,6},{6,2},{3,7},{7,3},{8,12},{12,8},{9,1... | collective-permute-start | bytes 3538952 | tf_op jit(solution)/shard_map/ppermute | solution.py:567
  799.9 43.5 %collective-permute-start.38 = (bf16[768,1536]{1,0:T(8,128)(2,1)}, bf16[768,1536]{1,0:T(8,128)(2,1)}, u32[]{:S(2)}, u32[]{:S(2)}) collective-permute-start(bf16[768,1536]{1,0:T(8,128)(2,1)} %fusion.53), channel_id=1, source_target_pairs={{0,2},{2,0},{1,3},{3,1},{4,6},{6,4},{5,7},{7,5},{8,10},{10,8},{9,1... | collective-permute-start | bytes 7077896 | tf_op jit(solution)/shard_map/ppermute | solution.py:567
  805.9 384.8 %reduce-scatter.11.cloned.1.call-start = ((), (), s32[]{:S(2)}) async-start(), calls=%async_computation.7 | async-start | bytes 2949120 | tf_op jit(solution)/shard_map/reduce_scatter | solution.py:634
  827.2 415.3 %collective-permute-start.34 = (bf16[768,1536]{1,0:T(8,128)(2,1)}, bf16[768,1536]{1,0:T(8,128)(2,1)}, u32[]{:S(2)}, u32[]{:S(2)}) collective-permute-start(bf16[768,1536]{1,0:T(8,128)(2,1)} %add_convert_fusion.1), channel_id=1, source_target_pairs={{1,2},{2,1},{5,6},{6,5},{9,10},{10,9},{13,14},{14,13},{17,18},{18,... | collective-permute-start | bytes 7077896 | tf_op jit(solution)/shard_map/ppermute | solution.py:766
  843.4 405.8 %reduce-scatter.5.cloned.1.call-start = ((), (), s32[]{:S(2)}) async-start(), calls=%async_computation.4 | async-start | bytes 2211840 | tf_op jit(solution)/shard_map/reduce_scatter | solution.py:634
  891.0 27.7 %collective-permute-start.57 = (bf16[768,384]{1,0:T(8,128)(2,1)S(1)}, bf16[768,384]{1,0:T(8,128)(2,1)}, u32[]{:S(2)}, u32[]{:S(2)}) collective-permute-start(bf16[768,384]{1,0:T(8,128)(2,1)S(1)} %bitcast.410), channel_id=1, source_target_pairs={{0,1},{1,0},{2,3},{3,2},{4,5},{5,4},{6,7},{7,6},{8,9},{9,8},{10,11... | collective-permute-start | bytes 1769480 | tf_op jit(solution)/shard_map/ppermute | solution.py:567
  913.1 52.3 %collective-permute-start.42 = (bf16[768,1536]{1,0:T(8,128)(2,1)S(1)}, bf16[768,1536]{1,0:T(8,128)(2,1)S(1)}, u32[]{:S(2)}, u32[]{:S(2)}) collective-permute-start(bf16[768,1536]{1,0:T(8,128)(2,1)S(1)} %fusion.148), channel_id=1, source_target_pairs={{0,2},{2,0},{1,3},{3,1},{4,6},{6,4},{5,7},{7,5},{8,10},{10,8},{9,1... | collective-permute-start | bytes 7077896 | tf_op jit(solution)/shard_map/ppermute | solution.py:567
  920.5 151.0 %collective-permute-start.63 = (bf16[768,768]{1,0:T(8,128)(2,1)}, bf16[768,768]{1,0:T(8,128)(2,1)}, u32[]{:S(2)}, u32[]{:S(2)}) collective-permute-start(bf16[768,768]{1,0:T(8,128)(2,1)} %bitcast.92), channel_id=1, source_target_pairs={{0,4},{4,0},{1,5},{5,1},{2,6},{6,2},{3,7},{7,3},{8,12},{12,8},{9,1... | collective-permute-start | bytes 3538952 | tf_op jit(solution)/shard_map/ppermute | solution.py:567
  931.4 31.6 %collective-permute-start.58 = (bf16[384,384]{1,0:T(8,128)(2,1)S(1)}, bf16[384,384]{1,0:T(8,128)(2,1)S(1)}, u32[]{:S(2)}, u32[]{:S(2)}) collective-permute-start(bf16[384,384]{1,0:T(8,128)(2,1)S(1)} %bitcast.420), channel_id=1, source_target_pairs={{0,4},{4,0},{1,5},{5,1},{2,6},{6,2},{3,7},{7,3},{8,12},{12,8},{9,1... | collective-permute-start | bytes 884744 | tf_op jit(solution)/shard_map/ppermute | solution.py:567
  963.0 115.5 %collective-permute-start.65 = (bf16[768,768]{1,0:T(8,128)(2,1)}, bf16[768,768]{1,0:T(8,128)(2,1)}, u32[]{:S(2)}, u32[]{:S(2)}) collective-permute-start(bf16[768,768]{1,0:T(8,128)(2,1)} %bitcast.99), channel_id=1, source_target_pairs={{0,1},{1,0},{2,3},{3,2},{4,5},{5,4},{6,7},{7,6},{8,9},{9,8},{10,11... | collective-permute-start | bytes 3538952 | tf_op jit(solution)/shard_map/ppermute | solution.py:567
  964.5 104.1 %collective-permute-start.62 = (bf16[384,384]{1,0:T(8,128)(2,1)}, bf16[384,384]{1,0:T(8,128)(2,1)}, u32[]{:S(2)}, u32[]{:S(2)}) collective-permute-start(bf16[384,384]{1,0:T(8,128)(2,1)} %bitcast.88), channel_id=1, source_target_pairs={{0,4},{4,0},{1,5},{5,1},{2,6},{6,2},{3,7},{7,3},{8,12},{12,8},{9,1... | collective-permute-start | bytes 884744 | tf_op jit(solution)/shard_map/ppermute | solution.py:567
  1060.2 38.8 %collective-permute-start.50 = (bf16[768,1152]{1,0:T(8,128)(2,1)S(1)}, bf16[768,1152]{1,0:T(8,128)(2,1)S(1)}, u32[]{:S(2)}, u32[]{:S(2)}) collective-permute-start(bf16[768,1152]{1,0:T(8,128)(2,1)S(1)} %bitcast.365), channel_id=1, source_target_pairs={{0,4},{4,0},{1,5},{5,1},{2,6},{6,2},{3,7},{7,3},{8,12},{12,8},{9,1... | collective-permute-start | bytes 5308424 | tf_op jit(solution)/shard_map/ppermute | solution.py:567
  1068.6 38.5 %collective-permute-start.52 = (bf16[768,1152]{1,0:T(8,128)(2,1)S(1)}, bf16[768,1152]{1,0:T(8,128)(2,1)S(1)}, u32[]{:S(2)}, u32[]{:S(2)}) collective-permute-start(bf16[768,1152]{1,0:T(8,128)(2,1)S(1)} %bitcast.366), channel_id=1, source_target_pairs={{0,1},{1,0},{2,3},{3,2},{4,5},{5,4},{6,7},{7,6},{8,9},{9,8},{10,11... | collective-permute-start | bytes 5308424 | tf_op jit(solution)/shard_map/ppermute | solution.py:567
  1071.5 171.0 %collective-permute-start.40 = (f32[64,1536]{1,0:T(8,128)}, f32[64,1536]{1,0:T(8,128)}, u32[]{:S(2)}, u32[]{:S(2)}) collective-permute-start(f32[64,1536]{1,0:T(8,128)} %add.396), channel_id=1, source_target_pairs={{1,2},{2,1},{5,6},{6,5},{9,10},{10,9},{13,14},{14,13},{17,18},{18,... | collective-permute-start | bytes 1179656 | tf_op jit(solution)/shard_map/ppermute | solution.py:766
  1078.5 83.9 %collective-permute-start.64 = (bf16[384,768]{1,0:T(8,128)(2,1)}, bf16[384,768]{1,0:T(8,128)(2,1)}, u32[]{:S(2)}, u32[]{:S(2)}) collective-permute-start(bf16[384,768]{1,0:T(8,128)(2,1)} %bitcast.95), channel_id=1, source_target_pairs={{0,1},{1,0},{2,3},{3,2},{4,5},{5,4},{6,7},{7,6},{8,9},{9,8},{10,11... | collective-permute-start | bytes 1769480 | tf_op jit(solution)/shard_map/ppermute | solution.py:567
  1099.5 44.4 %collective-permute-start.51 = (bf16[384,1152]{1,0:T(8,128)(2,1)S(1)}, bf16[384,1152]{1,0:T(8,128)(2,1)S(1)}, u32[]{:S(2)}, u32[]{:S(2)}) collective-permute-start(bf16[384,1152]{1,0:T(8,128)(2,1)S(1)} %bitcast.401), channel_id=1, source_target_pairs={{0,1},{1,0},{2,3},{3,2},{4,5},{5,4},{6,7},{7,6},{8,9},{9,8},{10,11... | collective-permute-start | bytes 2654216 | tf_op jit(solution)/shard_map/ppermute | solution.py:567
  1107.7 37.7 %collective-permute-start.53 = (bf16[384,1152]{1,0:T(8,128)(2,1)S(1)}, bf16[384,1152]{1,0:T(8,128)(2,1)S(1)}, u32[]{:S(2)}, u32[]{:S(2)}) collective-permute-start(bf16[384,1152]{1,0:T(8,128)(2,1)S(1)} %bitcast.402), channel_id=1, source_target_pairs={{0,4},{4,0},{1,5},{5,1},{2,6},{6,2},{3,7},{7,3},{8,12},{12,8},{9,1... | collective-permute-start | bytes 2654216 | tf_op jit(solution)/shard_map/ppermute | solution.py:567
  1147.0 104.6 %reduce-scatter.7.cloned.1.call-start = ((), (), s32[]{:S(2)}) async-start(), calls=%async_computation.5 | async-start | bytes 3686400 | tf_op jit(solution)/shard_map/reduce_scatter | solution.py:634
  1157.2 37.8 %collective-permute-start.43 = (bf16[768,1536]{1,0:T(8,128)(2,1)}, bf16[768,1536]{1,0:T(8,128)(2,1)}, u32[]{:S(2)}, u32[]{:S(2)}) collective-permute-start(bf16[768,1536]{1,0:T(8,128)(2,1)} %fusion.46), channel_id=1, source_target_pairs={{0,2},{2,0},{1,3},{3,1},{4,6},{6,4},{5,7},{7,5},{8,10},{10,8},{9,1... | collective-permute-start | bytes 7077896 | tf_op jit(solution)/shard_map/ppermute | solution.py:567
  1185.5 41.9 %collective-permute-start.76 = (bf16[96,3072]{1,0:T(8,128)(2,1)}, bf16[96,3072]{1,0:T(8,128)(2,1)}, u32[]{:S(2)}, u32[]{:S(2)}) collective-permute-start(bf16[96,3072]{1,0:T(8,128)(2,1)} %bitcast.404), channel_id=1, source_target_pairs={{1,2},{2,1},{5,6},{6,5},{9,10},{10,9},{13,14},{14,13},{17,18},{18,... | collective-permute-start | bytes 1769480 | tf_op jit(solution)/shard_map/ppermute | solution.py:562
  1190.7 43.5 %collective-permute-start.81 = (bf16[96,3072]{1,0:T(8,128)(2,1)}, bf16[96,3072]{1,0:T(8,128)(2,1)S(1)}, u32[]{:S(2)}, u32[]{:S(2)}) collective-permute-start(bf16[96,3072]{1,0:T(8,128)(2,1)} %bitcast.405), channel_id=1, source_target_pairs={{1,2},{2,1},{5,6},{6,5},{9,10},{10,9},{13,14},{14,13},{17,18},{18,... | collective-permute-start | bytes 1769480 | tf_op jit(solution)/shard_map/ppermute | solution.py:562
  1224.1 31.5 %collective-permute-start.49 = (bf16[768,1536]{1,0:T(8,128)(2,1)}, bf16[768,1536]{1,0:T(8,128)(2,1)S(1)}, u32[]{:S(2)}, u32[]{:S(2)}) collective-permute-start(bf16[768,1536]{1,0:T(8,128)(2,1)} %add_convert_fusion), channel_id=1, source_target_pairs={{1,2},{2,1},{5,6},{6,5},{9,10},{10,9},{13,14},{14,13},{17,18},{18,... | collective-permute-start | bytes 7077896 | tf_op jit(solution)/shard_map/ppermute | solution.py:562
  (154 other events, 3172.8 us)
Sparse Core Ops, SparseCore 0:
  44.5 44.4 all-gather.8
  118.1 59.5 all-gather.10
  185.3 48.5 all-gather.14
  320.8 47.0 all-gather.12
  806.0 45.3 reduce-scatter.8
  853.5 47.0 reduce-scatter.10
  1147.1 36.4 reduce-scatter.4
  1195.0 56.4 reduce-scatter.6
